TPU v7x, 128 devices: a whole 4x4x4 slice. The times are simulated.
128 devices in a mesh: elem: 32 (over x_hi, y, z), comp: 2 (over x_lo), rep: 2 (over core).
Axes of the slice: x: 4 (x_hi: 2, x_lo: 2; x = x_hi * 2 + x_lo), y: 4, z: 4, core: 2. Of those that a mesh axis runs over, the one named last changes fastest.
Arguments:
- velocity: float32 [3, 10, 10, 10, 2, 24576], P(None, 'comp', None, None, None, ('elem', 'rep')), may hold values from -6 to 6
- geometry: float32 [3, 3, 10, 10, 10, 2, 24576], P(None, None, 'comp', None, None, None, ('elem', 'rep')), may hold values from -40 to 40
- element_place: int32 [2, 24576], P('comp', ('elem', 'rep')), may hold values from 0 to 383, as said below
Outputs:
- pressure: float32 [10, 10, 10, 2, 24576], P(None, None, None, 'comp', ('elem', 'rep'))
Inputs may be any that keep to these rules, and one draw needn't show every extreme that they name: `element_place`: in each row and each aligned run of 384 entries of it, every value 0 to 383 appears once.
All inputs are finite; a program needn't handle non-finite values.
Results may differ from a plain program's by a relative error of at most 0.000071.
Values sent between devices are 32-bit elements; how exact they have to be, the bound alone decides.
A program may use at most 192 MiB of HBM per device.

v0:
```python
import jax
import jax.numpy as jnp
import numpy as np
from jax import lax
from jax.experimental import pallas as pl
from jax.experimental.pallas import tpu as pltpu
from jax.sharding import PartitionSpec as P

BLOCK_X = 6
BLOCK_Y = 8
BLOCK_Z = 8
GRID_Y = 4
NODES = 10
HALF = 5
ELEMS = 384
LANES = 128
TILES = 3
ROWS = 104
MESH = pl.DeviceIdType.MESH


def legendre_columns(points, degree):
    columns = [points * 0.0 + 1.0, points]
    for order in range(2, degree + 1):
        columns.append(
            ((2 * order - 1) * points * columns[order - 1] - (order - 1) * columns[order - 2])
            / order
        )
    return columns


def derivative_table(node_count):
    degree = node_count - 1
    points = np.cos(np.pi * np.arange(node_count) / degree)
    for sweep in range(100):
        columns = legendre_columns(points, degree)
        points = points - (points * columns[degree] - columns[degree - 1]) / (
            node_count * columns[degree]
        )
    points = np.sort(points)
    values = legendre_columns(points, degree)[degree]
    identity = np.eye(node_count)
    spacing = points[:, None] - points[None, :] + identity
    matrix = values[:, None] / (values[None, :] * spacing)
    matrix = np.where(identity > 0.5, 0.0, matrix)
    matrix[0, 0] = -degree * (degree + 1) / 4.0
    matrix[degree, degree] = degree * (degree + 1) / 4.0
    return matrix


TABLE = derivative_table(NODES)
EVEN = [[float(0.5 * (TABLE[i, m] + TABLE[i, 9 - m])) for m in range(HALF)] for i in range(HALF)]
ODD = [[float(0.5 * (TABLE[i, m] - TABLE[i, 9 - m])) for m in range(HALF)] for i in range(HALF)]


def weighted(terms, weights):
    total = terms[0] * weights[0]
    for term, weight in zip(terms[1:], weights[1:]):
        total = total + term * weight
    return total


def along(values):
    minus = [values[i] - values[9 - i] for i in range(HALF)]
    plus = [values[i] + values[9 - i] for i in range(HALF)]
    out = [None] * NODES
    for m in range(HALF):
        even = weighted(minus, [EVEN[i][m] for i in range(HALF)])
        odd = weighted(plus, [ODD[i][m] for i in range(HALF)])
        out[m] = even + odd
        out[9 - m] = even - odd
    return out


def tile(t):
    return slice(t * LANES, (t + 1) * LANES)


def roll_lanes(x, shift):
    return pltpu.roll(x, shift % LANES, 1)


def roll_rows(x, shift):
    return pltpu.roll(x, shift % 8, 0)


def two_parts(x):
    high = x.astype(jnp.bfloat16)
    low = (x - high.astype(jnp.float32)).astype(jnp.bfloat16)
    return jnp.concatenate([high, low], axis=1)


def kernel(
    v_hbm, g_hbm, place_ref, out_ref,
    v, g, coef, f0, fl, lhs, perm, back, place_in, canon, got,
    zs, zr, ys, yr, xs, xr, tops, tops_in,
    v_sem, g_sem, place_sem, z_sem, y_sem, x_sem, inner_send, inner_recv, edge_send, edge_recv,
):
    elem = lax.axis_index("elem")
    c = lax.axis_index("comp")
    r = lax.axis_index("rep")
    o = 1 - c
    elem_count = lax.axis_size("elem")
    grid_x = elem_count // GRID_Y
    sx = elem // GRID_Y
    sy = elem % GRID_Y
    y_up = sx * GRID_Y + (sy + 1) % GRID_Y
    y_down = sx * GRID_Y + (sy + GRID_Y - 1) % GRID_Y
    x_up = (elem + GRID_Y) % elem_count
    x_down = (elem + elem_count - GRID_Y) % elem_count

    for i in range(HALF):
        pltpu.make_async_copy(v_hbm.at[:, i], v.at[:, i], v_sem.at[i]).start()
        pltpu.make_async_copy(g_hbm.at[:, 0, i], g.at[:, 0, i], g_sem.at[0, i]).start()
    for i in range(HALF):
        for j in (1, 2):
            pltpu.make_async_copy(g_hbm.at[:, j, i], g.at[:, j, i], g_sem.at[j, i]).start()

    others = (
        (elem, o, r), (elem, c, 1 - r), (y_up, c, r), (y_down, c, r), (x_up, c, r), (x_down, c, r),
    )
    barrier = pltpu.get_barrier_semaphore()
    for other in others:
        pl.semaphore_signal(barrier, inc=1, device_id=other, device_id_type=MESH)

    for kind in range(2):
        for m in range(HALF):
            for i in range(HALF):
                first = float(TABLE[i, (5 + m) if kind == 0 else m])
                second = float(TABLE[5 + i, m if kind == 0 else (5 + m)])
                coef[(kind * HALF + m) * HALF + i] = jnp.where(c == 0, first, second).astype(jnp.float32)

    pl.semaphore_wait(barrier, len(others))
    place_copy = pltpu.make_async_remote_copy(
        src_ref=place_ref, dst_ref=place_in, send_sem=place_sem.at[0], recv_sem=place_sem.at[1],
        device_id=(elem, o, r), device_id_type=MESH,
    )
    place_copy.start()

    rows_iota = lax.broadcasted_iota(jnp.int32, (ELEMS, ELEMS), 0)
    hit = (rows_iota == place_ref[...]).astype(jnp.float32)
    back_half = hit.astype(jnp.bfloat16)
    back[0:ELEMS, :] = back_half
    back[ELEMS : 2 * ELEMS, :] = back_half
    own_half = hit.T.astype(jnp.bfloat16)
    perm[c, 0:ELEMS, :] = own_half
    perm[c, ELEMS : 2 * ELEMS, :] = own_half
    lhs[...] = jnp.zeros_like(lhs)

    def first_flux(i, carry):
        pltpu.make_async_copy(v_hbm.at[:, i], v.at[:, i], v_sem.at[i]).wait()
        pltpu.make_async_copy(g_hbm.at[:, 0, i], g.at[:, 0, i], g_sem.at[0, i]).wait()

        def at_b(b, carry):
            for k in range(NODES):
                f0[i, b, k] = (
                    g[0, 0, i, b, k] * v[0, i, b, k]
                    + g[1, 0, i, b, k] * v[1, i, b, k]
                    + g[2, 0, i, b, k] * v[2, i, b, k]
                )
            return carry

        return lax.fori_loop(0, NODES, at_b, carry)

    lax.fori_loop(0, HALF, first_flux, 0)

    place_copy.wait()
    hit_in = (rows_iota == place_in[...]).astype(jnp.float32)
    other_half = hit_in.T.astype(jnp.bfloat16)
    perm[o, 0:ELEMS, :] = other_half
    perm[o, ELEMS : 2 * ELEMS, :] = other_half

    def inner_copy(a):
        return pltpu.make_async_remote_copy(
            src_ref=canon.at[o, a, 0:64], dst_ref=got.at[a, 0:64],
            send_sem=inner_send.at[a], recv_sem=inner_recv.at[a],
            device_id=(elem, o, r), device_id_type=MESH,
        )

    def is_inner(a):
        return jnp.logical_and(a > 0, a < NODES - 1)

    def mix_planes(base, b):
        weights = [coef[base + i] for i in range(HALF)]
        for k in range(NODES):
            fl[b, k] = weighted([f0[i, b, k] for i in range(HALF)], weights)

    def gather_rows():
        for q in range(2):
            for t in range(TILES):
                for b in range(8):
                    lhs[q, b * 8 : b * 8 + 8, tile(t)] = fl[b + 1, 1:9, q, tile(t)]
                lhs[q, 64:72, tile(t)] = fl[1:9, 0, q, tile(t)]
                lhs[q, 72:80, tile(t)] = fl[0, 1:9, q, tile(t)]
                lhs[q, 80:88, tile(t)] = fl[1:9, 9, q, tile(t)]
                lhs[q, 88:96, tile(t)] = fl[9, 1:9, q, tile(t)]
            lhs[q, 96:97, :] = fl[0, 0, q : q + 1, :]
            lhs[q, 97:98, :] = fl[0, 9, q : q + 1, :]
            lhs[q, 98:99, :] = fl[9, 0, q : q + 1, :]
            lhs[q, 99:100, :] = fl[9, 9, q : q + 1, :]

    def to_canon(a):
        for q in range(2):
            canon[q, a] = jnp.dot(two_parts(lhs[q]), perm[q], preferred_element_type=jnp.float32)

    def send_if_inner(a):
        @pl.when(is_inner(a))
        def _():
            inner_copy(a).start()

    far = HALF * o
    near = HALF * c

    def far_plane(m, carry):
        def at_b(b, carry):
            mix_planes(m * HALF, b)
            return carry

        lax.fori_loop(0, NODES, at_b, 0)
        gather_rows()

        @pl.when(m > 0)
        def _():
            send_if_inner(far + m - 1)

        to_canon(far + m)
        return carry

    lax.fori_loop(0, HALF, far_plane, 0)

    def near_plane(m, carry):
        for j in (1, 2):
            pltpu.make_async_copy(g_hbm.at[:, j, m], g.at[:, j, m], g_sem.at[j, m]).wait()

        def flux(j, b, k):
            return (
                g[0, j, m, b, k] * v[0, m, b, k]
                + g[1, j, m, b, k] * v[1, m, b, k]
                + g[2, j, m, b, k] * v[2, m, b, k]
            )

        def at_b(b, carry):
            base = (HALF + m) * HALF
            weights = [coef[base + i] for i in range(HALF)]
            out = along([flux(2, b, k) for k in range(NODES)])
            for k in range(NODES):
                fl[b, k] = out[k] + weighted([f0[i, b, k] for i in range(HALF)], weights)
            return carry

        lax.fori_loop(0, NODES, at_b, 0)

        def at_k(k, carry):
            out = along([flux(1, b, k) for b in range(NODES)])
            for b in range(NODES):
                fl[b, k] = fl[b, k] + out[b]
            return carry

        lax.fori_loop(0, NODES, at_k, 0)
        gather_rows()

        @pl.when(m == 0)
        def _():
            send_if_inner(far + HALF - 1)

        @pl.when(m > 0)
        def _():
            send_if_inner(near + m - 1)

        to_canon(near + m)
        return carry

    lax.fori_loop(0, HALF, near_plane, 0)

    lane = lax.broadcasted_iota(jnp.int32, (8, LANES), 1)
    row = lax.broadcasted_iota(jnp.int32, (8, LANES), 0)
    zi = lane % 8
    yi = (lane // 8) % 8
    low_half = lane < 64
    zero = jnp.zeros((8, LANES), jnp.float32)
    c_lo = jnp.logical_or(row == 0, row == 2)
    c_hi = jnp.logical_or(row == 1, row == 3)
    b_lo = row < 2
    b_hi = jnp.logical_or(row == 2, row == 3)

    def yz_pass(a, carry):
        for q in range(2):
            for t in range(TILES):
                lo, hi = canon[q, a, 64:72, tile(t)], canon[q, a, 80:88, tile(t)]
                canon[q, a, 64:72, tile(t)] = lo + jnp.where(zi > 0, roll_lanes(hi, 1), zero)
                canon[q, a, 80:88, tile(t)] = hi + jnp.where(zi < 7, roll_lanes(lo, -1), zero)
                lo, hi = canon[q, a, 72:80, tile(t)], canon[q, a, 88:96, tile(t)]
                canon[q, a, 72:80, tile(t)] = lo + jnp.where(yi > 0, roll_lanes(hi, 8), zero)
                canon[q, a, 88:96, tile(t)] = hi + jnp.where(yi < 7, roll_lanes(lo, -8), zero)
                k = canon[q, a, 96:104, tile(t)]
                to_lo = jnp.where(jnp.logical_and(c_lo, zi > 0), roll_lanes(roll_rows(k, -1), 1), zero)
                to_hi = jnp.where(jnp.logical_and(c_hi, zi < 7), roll_lanes(roll_rows(k, 1), -1), zero)
                k = k + to_lo + to_hi
                to_lo = jnp.where(jnp.logical_and(b_lo, yi > 0), roll_lanes(roll_rows(k, -2), 8), zero)
                to_hi = jnp.where(jnp.logical_and(b_hi, yi < 7), roll_lanes(roll_rows(k, 2), -8), zero)
                canon[q, a, 96:104, tile(t)] = k + to_lo + to_hi
        return carry

    lax.fori_loop(0, NODES, yz_pass, 0)

    @pl.when(is_inner(near + HALF - 1))
    def _():
        inner_copy(near + HALF - 1).start()

    def x_pass(block, carry):
        here = pl.ds(pl.multiple_of(block * 8, 8), 8)
        for q in range(2):
            lo = [canon[q, 0, here, tile(t)] for t in range(TILES)]
            hi = [canon[q, 9, here, tile(t)] for t in range(TILES)]
            lo_rolled = [roll_lanes(x, 64) for x in lo] + [zero]
            hi_rolled = [roll_lanes(x, 64) for x in hi] + [zero]
            for t in range(TILES):
                canon[q, 0, here, tile(t)] = lo[t] + jnp.where(low_half, hi_rolled[t - 1], hi_rolled[t])
                canon[q, 9, here, tile(t)] = hi[t] + jnp.where(low_half, lo_rolled[t], lo_rolled[t + 1])
        return carry

    lax.fori_loop(0, ROWS // 8, x_pass, 0)

    def pack_top(parts, index, step):
        total = parts[0]
        for u in range(1, len(parts)):
            total = jnp.where(index == 7 - u, roll_lanes(parts[u], -step * u), total)
        return total

    def pack_low(parts, index, step):
        total = parts[0]
        for u in range(1, len(parts)):
            total = jnp.where(index == u, roll_lanes(parts[u], step * u), total)
        return total

    def six(a, rows):
        return [canon[q, a, rows, tile(t)] for q in range(2) for t in range(TILES)]

    def on(flag):
        return jnp.where(flag, 1.0, 0.0).astype(jnp.float32)

    def z_pack(a, carry):
        corner = six(a, slice(96, 104))
        zs[0, a, 0:8] = pack_top(six(a, slice(80, 88)), zi, 1)
        zs[0, a, 8:16] = pack_top(corner, zi, 1)
        zs[1, a, 0:8] = pack_low(six(a, slice(64, 72)), zi, 1)
        zs[1, a, 8:16] = pack_low(corner, zi, 1)
        return carry

    lax.fori_loop(0, NODES, z_pack, 0)
    z_copy = pltpu.make_async_remote_copy(
        src_ref=zs, dst_ref=zr, send_sem=z_sem.at[0], recv_sem=z_sem.at[1],
        device_id=(elem, c, 1 - r), device_id_type=MESH,
    )
    z_copy.start()

    def put(a, b_row, value, t, first):
        start = ((a * 10 + b_row) * 10 + 1) * 3 + t
        out_ref[pl.ds(start, 8, stride=3), :] = value[first : first + 8, tile(t)]

    def put_column(a, k_row, value, t, first):
        start = ((a * 10 + 1) * 10 + k_row) * 3 + t
        out_ref[pl.ds(start, 8, stride=30), :] = value[first : first + 8, tile(t)]

    def put_edges(a, value, first):
        for t in range(TILES):
            put_column(a, 0, value, t, first)
            put(a, 0, value, t, first + 8)
            put_column(a, 9, value, t, first + 16)
            put(a, 9, value, t, first + 24)
            for number, (b, k) in enumerate(((0, 0), (0, 9), (9, 0), (9, 9))):
                start = ((a * 10 + b) * 10 + k) * 3 + t
                out_ref[pl.ds(start, 1), :] = value[first + 32 + number : first + 33 + number, tile(t)]

    def inner_done(a, carry):
        @pl.when(is_inner(a))
        def _():
            inner_copy(a).wait_recv()
            total = canon[c, a, 0:64] + got[a, 0:64]
            value = jnp.dot(two_parts(total), back[...], preferred_element_type=jnp.float32)
            for t in range(TILES):
                for b in range(8):
                    put(a, b + 1, value, t, b * 8)

        return carry

    lax.fori_loop(near, near + 2, inner_done, 0)

    z_copy.wait_recv()
    r0, r1 = on(r == 0), on(r == 1)

    def z_unpack(a, carry):
        tops_here = [zr[0, a, 0:8], roll_rows(zr[0, a, 8:16], -1)]
        lows_here = [zr[1, a, 0:8], roll_rows(zr[1, a, 8:16], 1)]
        for t in range(TILES):
            for kind in range(2):
                top_rows = slice(80, 88) if kind == 0 else slice(96, 104)
                low_rows = slice(64, 72) if kind == 0 else slice(96, 104)
                top_mask = zi == 7 if kind == 0 else jnp.logical_and(c_hi, zi == 7)
                low_mask = zi == 0 if kind == 0 else jnp.logical_and(c_lo, zi == 0)
                from_above = [roll_lanes(lows_here[kind], 7 - (3 * q + t)) for q in range(2)]
                from_below = [roll_lanes(tops_here[kind], 3 * q + t - 7) for q in range(2)]
                adds = (
                    (0, top_rows, top_mask, from_above[0] * r0 + from_above[1] * r1),
                    (1, top_rows, top_mask, from_above[1] * r0),
                    (0, low_rows, low_mask, from_below[0] * r1),
                    (1, low_rows, low_mask, from_below[0] * r0 + from_below[1] * r1),
                )
                for q, rows, mask, value in adds:
                    canon[q, a, rows, tile(t)] = canon[q, a, rows, tile(t)] + jnp.where(mask, value, zero)
        return carry

    lax.fori_loop(0, NODES, z_unpack, 0)

    def y_pack(a, carry):
        corner = six(a, slice(96, 104))
        ys[0, a, 0:8] = pack_top(six(a, slice(88, 96)), yi, 8)
        ys[0, a, 8:16] = pack_top(corner, yi, 8)
        ys[1, a, 0:8] = pack_low(six(a, slice(72, 80)), yi, 8)
        ys[1, a, 8:16] = pack_low(corner, yi, 8)
        return carry

    lax.fori_loop(0, NODES, y_pack, 0)
    y_copies = [
        pltpu.make_async_remote_copy(
            src_ref=ys.at[way], dst_ref=yr.at[way], send_sem=y_sem.at[0, way], recv_sem=y_sem.at[1, way],
            device_id=(y_up if way == 0 else y_down, c, r), device_id_type=MESH,
        )
        for way in range(2)
    ]
    for copy in y_copies:
        copy.start()

    lax.fori_loop(near + 2, near + 4, inner_done, 0)

    for copy in y_copies:
        copy.wait_recv()
    y_has_up, y_has_down = on(sy < GRID_Y - 1), on(sy > 0)

    def y_unpack(a, carry):
        below = [yr[0, a, 0:8] * y_has_down, roll_rows(yr[0, a, 8:16], -2) * y_has_down]
        above = [yr[1, a, 0:8] * y_has_up, roll_rows(yr[1, a, 8:16], 2) * y_has_up]
        for q in range(2):
            for t in range(TILES):
                u = 3 * q + t
                for kind in range(2):
                    top_rows = slice(88, 96) if kind == 0 else slice(96, 104)
                    low_rows = slice(72, 80) if kind == 0 else slice(96, 104)
                    top_mask = yi == 7 if kind == 0 else jnp.logical_and(b_hi, yi == 7)
                    low_mask = yi == 0 if kind == 0 else jnp.logical_and(b_lo, yi == 0)
                    up = jnp.where(top_mask, roll_lanes(above[kind], 8 * (7 - u)), zero)
                    down = jnp.where(low_mask, roll_lanes(below[kind], 8 * (u - 7)), zero)
                    canon[q, a, top_rows, tile(t)] = canon[q, a, top_rows, tile(t)] + up
                    canon[q, a, low_rows, tile(t)] = canon[q, a, low_rows, tile(t)] + down
        return carry

    lax.fori_loop(0, NODES, y_unpack, 0)

    def x_pack(block, carry):
        here = pl.ds(pl.multiple_of(block * 8, 8), 8)
        xs[0, here] = jnp.where(low_half, roll_lanes(canon[0, 9, here, tile(2)], 64), canon[1, 9, here, tile(2)])
        xs[1, here] = jnp.where(low_half, canon[0, 0, here, tile(0)], roll_lanes(canon[1, 0, here, tile(0)], 64))
        return carry

    lax.fori_loop(0, ROWS // 8, x_pack, 0)
    x_copies = [
        pltpu.make_async_remote_copy(
            src_ref=xs.at[way], dst_ref=xr.at[way], send_sem=x_sem.at[0, way], recv_sem=x_sem.at[1, way],
            device_id=(x_up if way == 0 else x_down, c, r), device_id_type=MESH,
        )
        for way in range(2)
    ]
    for copy in x_copies:
        copy.start()

    def edge_copy(number, source, target):
        return pltpu.make_async_remote_copy(
            src_ref=source, dst_ref=target, send_sem=edge_send.at[number], recv_sem=edge_recv.at[number],
            device_id=(elem, o, r), device_id_type=MESH,
        )

    edges = [
        edge_copy(0, canon.at[o, 1:9, 64:80], got.at[1:9, 64:80]),
        edge_copy(1, canon.at[o, 1:9, 96:104], got.at[1:9, 96:104]),
        edge_copy(2, tops.at[1:9], tops_in.at[1:9]),
        edge_copy(3, tops.at[0], tops_in.at[0]),
        edge_copy(4, canon.at[o, 0, 0:80], got.at[0, 0:80]),
        edge_copy(5, canon.at[o, 0, 96:104], got.at[0, 96:104]),
        edge_copy(6, canon.at[o, 9, :, 256:384], got.at[9, :, 256:384]),
    ]

    def fill_tops(a, carry):
        tops[a, 0:8] = pack_top([canon[o, a, 80:88, tile(t)] for t in range(TILES)], zi, 1)
        tops[a, 8:16] = pack_top([canon[o, a, 88:96, tile(t)] for t in range(TILES)], yi, 8)
        return carry

    edges[0].start()
    edges[1].start()
    lax.fori_loop(1, NODES - 1, fill_tops, 0)
    lax.fori_loop(near + 4, near + 5, inner_done, 0)
    edges[2].start()

    for copy in x_copies:
        copy.wait_recv()
    x_has_up, x_has_down = on(sx < grid_x - 1), on(sx > 0)

    def x_unpack(block, carry):
        here = pl.ds(pl.multiple_of(block * 8, 8), 8)
        below = xr[0, here] * x_has_down
        above = xr[1, here] * x_has_up
        low = (jnp.where(low_half, below, zero), jnp.where(low_half, roll_lanes(below, 64), zero))
        top = (jnp.where(low_half, zero, roll_lanes(above, 64)), jnp.where(low_half, zero, above))
        for q in range(2):
            canon[q, 0, here, tile(0)] = canon[q, 0, here, tile(0)] + low[q]
            canon[q, 9, here, tile(2)] = canon[q, 9, here, tile(2)] + top[q]
        return carry

    lax.fori_loop(0, ROWS // 8, x_unpack, 0)
    fill_tops(0, 0)
    edges[4].start()
    edges[5].start()
    lax.fori_loop(far, far + 1, inner_done, 0)
    edges[3].start()
    edges[6].start()
    lax.fori_loop(far + 1, far + 5, inner_done, 0)

    def complete(a, carry):
        for t in range(TILES):
            top = tops_in[a, 0:8]
            lo = got[a, 64:72, tile(t)]
            got[a, 80:88, tile(t)] = jnp.where(zi < 7, roll_lanes(lo, -1), roll_lanes(top, t))
            top = tops_in[a, 8:16]
            lo = got[a, 72:80, tile(t)]
            got[a, 88:96, tile(t)] = jnp.where(yi < 7, roll_lanes(lo, -8), roll_lanes(top, 8 * t))
        return carry

    for number in range(3):
        edges[number].wait_recv()
    lax.fori_loop(1, NODES - 1, complete, 0)

    def pair_done(pair, carry):
        start = 1 + pair * 4
        total = canon[c, pl.ds(start, 4), 64:104] + got[pl.ds(start, 4), 64:104]
        value = jnp.dot(
            two_parts(total.reshape(160, ELEMS)), back[...], preferred_element_type=jnp.float32
        )
        for k in range(4):
            put_edges(start + k, value, k * 40)
        return carry

    lax.fori_loop(0, 2, pair_done, 0)

    for number in range(3, 7):
        edges[number].wait_recv()
    complete(0, 0)

    def last_plane(block, carry):
        here = pl.ds(pl.multiple_of(block * 8, 8), 8)
        lo = [roll_lanes(got[0, here, tile(t)], 64) for t in range(TILES)]
        for t in range(TILES):
            after = lo[t + 1] if t < TILES - 1 else got[9, here, tile(2)]
            got[9, here, tile(t)] = jnp.where(low_half, lo[t], after)
        return carry

    lax.fori_loop(0, ROWS // 8, last_plane, 0)

    for a in (0, 9):
        total = canon[c, a] + got[a]
        value = jnp.dot(two_parts(total), back[...], preferred_element_type=jnp.float32)
        for t in range(TILES):
            for b in range(8):
                put(a, b + 1, value, t, b * 8)
        put_edges(a, value, 64)

    z_copy.wait_send()
    for copy in y_copies + x_copies + edges:
        copy.wait_send()

    def sent(a, carry):
        inner_copy(a).wait_send()
        return carry

    lax.fori_loop(1, NODES - 1, sent, 0)


def body(velocity, geometry, element_place):
    vmem = pltpu.VMEM
    dma = pltpu.SemaphoreType.DMA
    f32 = jnp.float32
    out = pl.pallas_call(
        kernel,
        out_shape=jax.ShapeDtypeStruct((NODES * NODES * NODES * TILES, LANES), f32),
        in_specs=[
            pl.BlockSpec(memory_space=pl.ANY),
            pl.BlockSpec(memory_space=pl.ANY),
            pl.BlockSpec(memory_space=pltpu.VMEM),
        ],
        out_specs=pl.BlockSpec(memory_space=pltpu.VMEM),
        scratch_shapes=[
            vmem((3, HALF, NODES, NODES, 2, ELEMS), f32),
            vmem((3, 3, HALF, NODES, NODES, 2, ELEMS), f32),
            pltpu.SMEM((2 * HALF * HALF,), f32),
            vmem((HALF, NODES, NODES, 2, ELEMS), f32),
            vmem((NODES, NODES, 2, ELEMS), f32),
            vmem((2, ROWS, ELEMS), f32),
            vmem((2, 2 * ELEMS, ELEMS), jnp.bfloat16),
            vmem((2 * ELEMS, ELEMS), jnp.bfloat16),
            vmem((1, ELEMS), jnp.int32),
            vmem((2, NODES, ROWS, ELEMS), f32),
            vmem((NODES, ROWS, ELEMS), f32),
            vmem((2, NODES, 16, LANES), f32),
            vmem((2, NODES, 16, LANES), f32),
            vmem((2, NODES, 16, LANES), f32),
            vmem((2, NODES, 16, LANES), f32),
            vmem((2, ROWS, LANES), f32),
            vmem((2, ROWS, LANES), f32),
            vmem((NODES - 1, 16, LANES), f32),
            vmem((NODES - 1, 16, LANES), f32),
            dma((HALF,)), dma((3, HALF)), dma((2,)), dma((2,)), dma((2, 2)), dma((2, 2)),
            dma((NODES,)), dma((NODES,)), dma((7,)), dma((7,)),
        ],
        compiler_params=pltpu.CompilerParams(
            collective_id=0, has_side_effects=True, vmem_limit_bytes=60 * 1024 * 1024
        ),
    )(velocity, geometry, element_place)
    return out.reshape(NODES, NODES, NODES, 1, ELEMS)


def solution(mesh):
    placed = (
        P(None, "comp", None, None, None, ("elem", "rep")),
        P(None, None, "comp", None, None, None, ("elem", "rep")),
        P("comp", ("elem", "rep")),
    )
    return jax.shard_map(
        body,
        mesh=mesh,
        in_specs=placed,
        out_specs=P(None, None, None, "comp", ("elem", "rep")),
        check_vma=False,
    )
```

profile of v0, /device:TPU:1, one launch (start us, length us, event | category | flops | bytes accessed | tf_op | source)
XLA Modules:
  0.0 57.5 jit_solution(15394577949918132547)
XLA Ops:
  0.0 53.9 %shard_map.37 = f32[3000,128]{1,0:T(8,128)} custom-call(f32[3,5,10,10,2,384]{5,4,3,2,1,0:T(2,128)} %v_hbm.1, f32[3,3,5,10,10,2,384]{6,5,4,3,2,1,0:T(2,128)} %g_hbm.1, s32[1,384]{1,0:T(1,128)} %place_ref.1), custom_call_target="tpu_custom_call" | custom-call | tf_op jit(solution)/shard_map/pallas_call | solution.py:589
  53.9 3.6 %copy.7 = f32[10,10,10,1,384]{4,3,2,1,0:T(1,128)} copy(f32[10,10,10,1,384]{4,3,2,1,0:T(1,128)} %bitcast.1) | data formatting | bytes 3072000
where the time goes:
time: 57.7 us; the launch traced here: 57.5 us
  Pallas kernels  53.9 us (93%)
  local copies, waits for them, and re-layouts  3.58 us (6%)
    pallas_call x1, Pallas kernels, body(): pl.pallas_call(kernel, out_shape=jax.ShapeDtypeStruct((NODES * NODES * NO...  53.9 us
    unnamed x1, local copies, waits for them, and re-layouts  3.58 us

commit v1 on v0

--- a/solution.py
+++ b/solution.py
@@ -90,10 +90,24 @@
     return jnp.concatenate([high, low], axis=1)
 
 
+def steps(start, count, per, fn):
+    if per == count:
+        for k in range(count):
+            fn(start + k, 0)
+        return
+
+    def several(step, carry):
+        for k in range(per):
+            fn(start + step * per + k, 0)
+        return carry
+
+    lax.fori_loop(0, count // per, several, 0)
+
+
 def kernel(
     v_hbm, g_hbm, place_ref, out_ref,
     v, g, coef, f0, fl, lhs, perm, back, place_in, canon, got,
-    zs, zr, ys, yr, xs, xr, tops, tops_in,
+    zs, zr, ys, yr, xs, xr, tops, tops_in, ends, ends_in,
     v_sem, g_sem, place_sem, z_sem, y_sem, x_sem, inner_send, inner_recv, edge_send, edge_recv,
 ):
     elem = lax.axis_index("elem")
@@ -112,10 +126,6 @@
     for i in range(HALF):
         pltpu.make_async_copy(v_hbm.at[:, i], v.at[:, i], v_sem.at[i]).start()
         pltpu.make_async_copy(g_hbm.at[:, 0, i], g.at[:, 0, i], g_sem.at[0, i]).start()
-    for i in range(HALF):
-        for j in (1, 2):
-            pltpu.make_async_copy(g_hbm.at[:, j, i], g.at[:, j, i], g_sem.at[j, i]).start()
-
     others = (
         (elem, o, r), (elem, c, 1 - r), (y_up, c, r), (y_down, c, r), (x_up, c, r), (x_down, c, r),
     )
@@ -130,6 +140,23 @@
                 second = float(TABLE[5 + i, m if kind == 0 else (5 + m)])
                 coef[(kind * HALF + m) * HALF + i] = jnp.where(c == 0, first, second).astype(jnp.float32)
 
+    rows_iota = lax.broadcasted_iota(jnp.int32, (ELEMS, ELEMS), 0)
+    lanes_iota = lax.broadcasted_iota(jnp.int32, (LANES, ELEMS), 1).astype(jnp.float32)
+
+    def fill_perm(q, places):
+        for t in range(TILES):
+            place = jnp.broadcast_to(places[:, tile(t)].astype(jnp.float32), (LANES, LANES)).T
+            place = jnp.concatenate([place] * TILES, axis=1)
+            part = jnp.where(lanes_iota == place, 1.0, 0.0).astype(jnp.bfloat16)
+            for copy in range(2):
+                perm[q, copy * ELEMS + t * LANES : copy * ELEMS + (t + 1) * LANES, :] = part
+
+    back_half = jnp.where(rows_iota == place_ref[...], 1.0, 0.0).astype(jnp.bfloat16)
+    back[0:ELEMS, :] = back_half
+    back[ELEMS : 2 * ELEMS, :] = back_half
+    fill_perm(c, place_ref[...])
+    lhs[...] = jnp.zeros_like(lhs)
+
     pl.semaphore_wait(barrier, len(others))
     place_copy = pltpu.make_async_remote_copy(
         src_ref=place_ref, dst_ref=place_in, send_sem=place_sem.at[0], recv_sem=place_sem.at[1],
@@ -137,19 +164,11 @@
     )
     place_copy.start()
 
-    rows_iota = lax.broadcasted_iota(jnp.int32, (ELEMS, ELEMS), 0)
-    hit = (rows_iota == place_ref[...]).astype(jnp.float32)
-    back_half = hit.astype(jnp.bfloat16)
-    back[0:ELEMS, :] = back_half
-    back[ELEMS : 2 * ELEMS, :] = back_half
-    own_half = hit.T.astype(jnp.bfloat16)
-    perm[c, 0:ELEMS, :] = own_half
-    perm[c, ELEMS : 2 * ELEMS, :] = own_half
-    lhs[...] = jnp.zeros_like(lhs)
-
     def first_flux(i, carry):
         pltpu.make_async_copy(v_hbm.at[:, i], v.at[:, i], v_sem.at[i]).wait()
         pltpu.make_async_copy(g_hbm.at[:, 0, i], g.at[:, 0, i], g_sem.at[0, i]).wait()
+        for j in (1, 2):
+            pltpu.make_async_copy(g_hbm.at[:, j, i], g.at[:, j, i], g_sem.at[j, i]).start()
 
         def at_b(b, carry):
             for k in range(NODES):
@@ -160,15 +179,13 @@
                 )
             return carry
 
-        return lax.fori_loop(0, NODES, at_b, carry)
+        steps(0, NODES, 2, at_b)
+        return carry
 
     lax.fori_loop(0, HALF, first_flux, 0)
 
     place_copy.wait()
-    hit_in = (rows_iota == place_in[...]).astype(jnp.float32)
-    other_half = hit_in.T.astype(jnp.bfloat16)
-    perm[o, 0:ELEMS, :] = other_half
-    perm[o, ELEMS : 2 * ELEMS, :] = other_half
+    fill_perm(o, place_in[...])
 
     def inner_copy(a):
         return pltpu.make_async_remote_copy(
@@ -200,7 +217,7 @@
             lhs[q, 99:100, :] = fl[9, 9, q : q + 1, :]
 
     def to_canon(a):
-        for q in range(2):
+        for q in (o, c):
             canon[q, a] = jnp.dot(two_parts(lhs[q]), perm[q], preferred_element_type=jnp.float32)
 
     def send_if_inner(a):
@@ -216,14 +233,10 @@
             mix_planes(m * HALF, b)
             return carry
 
-        lax.fori_loop(0, NODES, at_b, 0)
+        steps(0, NODES, 2, at_b)
         gather_rows()
-
-        @pl.when(m > 0)
-        def _():
-            send_if_inner(far + m - 1)
-
         to_canon(far + m)
+        send_if_inner(far + m)
         return carry
 
     lax.fori_loop(0, HALF, far_plane, 0)
@@ -247,7 +260,7 @@
                 fl[b, k] = out[k] + weighted([f0[i, b, k] for i in range(HALF)], weights)
             return carry
 
-        lax.fori_loop(0, NODES, at_b, 0)
+        steps(0, NODES, 2, at_b)
 
         def at_k(k, carry):
             out = along([flux(1, b, k) for b in range(NODES)])
@@ -255,18 +268,10 @@
                 fl[b, k] = fl[b, k] + out[b]
             return carry
 
-        lax.fori_loop(0, NODES, at_k, 0)
+        steps(0, NODES, 2, at_k)
         gather_rows()
-
-        @pl.when(m == 0)
-        def _():
-            send_if_inner(far + HALF - 1)
-
-        @pl.when(m > 0)
-        def _():
-            send_if_inner(near + m - 1)
-
         to_canon(near + m)
+        send_if_inner(near + m)
         return carry
 
     lax.fori_loop(0, HALF, near_plane, 0)
@@ -282,32 +287,45 @@
     b_lo = row < 2
     b_hi = jnp.logical_or(row == 2, row == 3)
 
-    def yz_pass(a, carry):
-        for q in range(2):
-            for t in range(TILES):
-                lo, hi = canon[q, a, 64:72, tile(t)], canon[q, a, 80:88, tile(t)]
-                canon[q, a, 64:72, tile(t)] = lo + jnp.where(zi > 0, roll_lanes(hi, 1), zero)
-                canon[q, a, 80:88, tile(t)] = hi + jnp.where(zi < 7, roll_lanes(lo, -1), zero)
-                lo, hi = canon[q, a, 72:80, tile(t)], canon[q, a, 88:96, tile(t)]
-                canon[q, a, 72:80, tile(t)] = lo + jnp.where(yi > 0, roll_lanes(hi, 8), zero)
-                canon[q, a, 88:96, tile(t)] = hi + jnp.where(yi < 7, roll_lanes(lo, -8), zero)
-                k = canon[q, a, 96:104, tile(t)]
-                to_lo = jnp.where(jnp.logical_and(c_lo, zi > 0), roll_lanes(roll_rows(k, -1), 1), zero)
-                to_hi = jnp.where(jnp.logical_and(c_hi, zi < 7), roll_lanes(roll_rows(k, 1), -1), zero)
-                k = k + to_lo + to_hi
-                to_lo = jnp.where(jnp.logical_and(b_lo, yi > 0), roll_lanes(roll_rows(k, -2), 8), zero)
-                to_hi = jnp.where(jnp.logical_and(b_hi, yi < 7), roll_lanes(roll_rows(k, 2), -8), zero)
-                canon[q, a, 96:104, tile(t)] = k + to_lo + to_hi
-        return carry
-
-    lax.fori_loop(0, NODES, yz_pass, 0)
-
-    @pl.when(is_inner(near + HALF - 1))
-    def _():
-        inner_copy(near + HALF - 1).start()
+    def edge_pass(step, carry):
+        spots = [
+            (q, 2 * step + k, lo_row, hi_row, tile(t))
+            for k in range(2) for q in range(2) for t in range(TILES) for lo_row, hi_row in ((64, 80), (72, 88))
+        ]
+        held = [
+            (canon[q, a, lo_row : lo_row + 8, lanes], canon[q, a, hi_row : hi_row + 8, lanes])
+            for q, a, lo_row, hi_row, lanes in spots
+        ]
+        for (q, a, lo_row, hi_row, lanes), (lo, hi) in zip(spots, held):
+            index, shift = (zi, 1) if lo_row == 64 else (yi, 8)
+            canon[q, a, lo_row : lo_row + 8, lanes] = lo + jnp.where(index > 0, roll_lanes(hi, shift), zero)
+            canon[q, a, hi_row : hi_row + 8, lanes] = hi + jnp.where(index < 7, roll_lanes(lo, -shift), zero)
+        return carry
+
+    def corner_pass(step, carry):
+        spots = [(q, 5 * step + k, tile(t)) for k in range(5) for q in range(2) for t in range(TILES)]
+        held = [canon[q, a, 96:104, lanes] for q, a, lanes in spots]
+        held = [
+            k
+            + jnp.where(jnp.logical_and(c_lo, zi > 0), roll_lanes(roll_rows(k, -1), 1), zero)
+            + jnp.where(jnp.logical_and(c_hi, zi < 7), roll_lanes(roll_rows(k, 1), -1), zero)
+            for k in held
+        ]
+        held = [
+            k
+            + jnp.where(jnp.logical_and(b_lo, yi > 0), roll_lanes(roll_rows(k, -2), 8), zero)
+            + jnp.where(jnp.logical_and(b_hi, yi < 7), roll_lanes(roll_rows(k, 2), -8), zero)
+            for k in held
+        ]
+        for (q, a, lanes), k in zip(spots, held):
+            canon[q, a, 96:104, lanes] = k
+        return carry
+
+    lax.fori_loop(0, NODES // 2, edge_pass, 0)
+    lax.fori_loop(0, 2, corner_pass, 0)
 
     def x_pass(block, carry):
-        here = pl.ds(pl.multiple_of(block * 8, 8), 8)
+        here = pl.ds(block * 8, 8)
         for q in range(2):
             lo = [canon[q, 0, here, tile(t)] for t in range(TILES)]
             hi = [canon[q, 9, here, tile(t)] for t in range(TILES)]
@@ -318,7 +336,7 @@
                 canon[q, 9, here, tile(t)] = hi[t] + jnp.where(low_half, lo_rolled[t], lo_rolled[t + 1])
         return carry
 
-    lax.fori_loop(0, ROWS // 8, x_pass, 0)
+    steps(0, ROWS // 8, 13, x_pass)
 
     def pack_top(parts, index, step):
         total = parts[0]
@@ -346,7 +364,7 @@
         zs[1, a, 8:16] = pack_low(corner, zi, 1)
         return carry
 
-    lax.fori_loop(0, NODES, z_pack, 0)
+    steps(0, NODES, NODES, z_pack)
     z_copy = pltpu.make_async_remote_copy(
         src_ref=zs, dst_ref=zr, send_sem=z_sem.at[0], recv_sem=z_sem.at[1],
         device_id=(elem, c, 1 - r), device_id_type=MESH,
@@ -409,7 +427,7 @@
                     canon[q, a, rows, tile(t)] = canon[q, a, rows, tile(t)] + jnp.where(mask, value, zero)
         return carry
 
-    lax.fori_loop(0, NODES, z_unpack, 0)
+    steps(0, NODES, NODES, z_unpack)
 
     def y_pack(a, carry):
         corner = six(a, slice(96, 104))
@@ -419,7 +437,7 @@
         ys[1, a, 8:16] = pack_low(corner, yi, 8)
         return carry
 
-    lax.fori_loop(0, NODES, y_pack, 0)
+    steps(0, NODES, NODES, y_pack)
     y_copies = [
         pltpu.make_async_remote_copy(
             src_ref=ys.at[way], dst_ref=yr.at[way], send_sem=y_sem.at[0, way], recv_sem=y_sem.at[1, way],
@@ -453,15 +471,15 @@
                     canon[q, a, low_rows, tile(t)] = canon[q, a, low_rows, tile(t)] + down
         return carry
 
-    lax.fori_loop(0, NODES, y_unpack, 0)
+    steps(0, NODES, NODES, y_unpack)
 
     def x_pack(block, carry):
-        here = pl.ds(pl.multiple_of(block * 8, 8), 8)
+        here = pl.ds(block * 8, 8)
         xs[0, here] = jnp.where(low_half, roll_lanes(canon[0, 9, here, tile(2)], 64), canon[1, 9, here, tile(2)])
         xs[1, here] = jnp.where(low_half, canon[0, 0, here, tile(0)], roll_lanes(canon[1, 0, here, tile(0)], 64))
         return carry
 
-    lax.fori_loop(0, ROWS // 8, x_pack, 0)
+    steps(0, ROWS // 8, 13, x_pack)
     x_copies = [
         pltpu.make_async_remote_copy(
             src_ref=xs.at[way], dst_ref=xr.at[way], send_sem=x_sem.at[0, way], recv_sem=x_sem.at[1, way],
@@ -480,31 +498,33 @@
 
     edges = [
         edge_copy(0, canon.at[o, 1:9, 64:80], got.at[1:9, 64:80]),
-        edge_copy(1, canon.at[o, 1:9, 96:104], got.at[1:9, 96:104]),
-        edge_copy(2, tops.at[1:9], tops_in.at[1:9]),
+        edge_copy(1, tops.at[1:9], tops_in.at[1:9]),
+        edge_copy(2, canon.at[o, 0, 0:80], got.at[0, 0:80]),
         edge_copy(3, tops.at[0], tops_in.at[0]),
-        edge_copy(4, canon.at[o, 0, 0:80], got.at[0, 0:80]),
-        edge_copy(5, canon.at[o, 0, 96:104], got.at[0, 96:104]),
-        edge_copy(6, canon.at[o, 9, :, 256:384], got.at[9, :, 256:384]),
+        edge_copy(4, ends, ends_in),
     ]
 
     def fill_tops(a, carry):
         tops[a, 0:8] = pack_top([canon[o, a, 80:88, tile(t)] for t in range(TILES)], zi, 1)
         tops[a, 8:16] = pack_top([canon[o, a, 88:96, tile(t)] for t in range(TILES)], yi, 8)
+        corner = [canon[o, a, 96:104, tile(t)] for t in range(TILES)]
+        packed = jnp.where(row < 2, pack_top(corner, zi, 1), pack_top(corner, yi, 8))
+        for t in range(TILES):
+            packed = jnp.where(row == 4 + t, roll_rows(corner[t], 4 + t), packed)
+        tops[a, 16:24] = packed
         return carry
 
     edges[0].start()
+    steps(1, NODES - 2, NODES - 2, fill_tops)
+    lax.fori_loop(near + 4, near + 5, inner_done, 0)
     edges[1].start()
-    lax.fori_loop(1, NODES - 1, fill_tops, 0)
-    lax.fori_loop(near + 4, near + 5, inner_done, 0)
-    edges[2].start()
 
     for copy in x_copies:
         copy.wait_recv()
     x_has_up, x_has_down = on(sx < grid_x - 1), on(sx > 0)
 
     def x_unpack(block, carry):
-        here = pl.ds(pl.multiple_of(block * 8, 8), 8)
+        here = pl.ds(block * 8, 8)
         below = xr[0, here] * x_has_down
         above = xr[1, here] * x_has_up
         low = (jnp.where(low_half, below, zero), jnp.where(low_half, roll_lanes(below, 64), zero))
@@ -514,13 +534,15 @@
             canon[q, 9, here, tile(2)] = canon[q, 9, here, tile(2)] + top[q]
         return carry
 
-    lax.fori_loop(0, ROWS // 8, x_unpack, 0)
+    steps(0, ROWS // 8, 13, x_unpack)
+    edges[2].start()
     fill_tops(0, 0)
-    edges[4].start()
-    edges[5].start()
+    blocks = [canon[o, 9, k * 8 : k * 8 + 8, tile(2)] for k in range(ROWS // 8)] + [zero]
+    for k in range(7):
+        ends[k * 8 : k * 8 + 8] = jnp.where(low_half, roll_lanes(blocks[k], 64), blocks[k + 7])
     lax.fori_loop(far, far + 1, inner_done, 0)
     edges[3].start()
-    edges[6].start()
+    edges[4].start()
     lax.fori_loop(far + 1, far + 5, inner_done, 0)
 
     def complete(a, carry):
@@ -531,11 +553,17 @@
             top = tops_in[a, 8:16]
             lo = got[a, 72:80, tile(t)]
             got[a, 88:96, tile(t)] = jnp.where(yi < 7, roll_lanes(lo, -8), roll_lanes(top, 8 * t))
-        return carry
-
-    for number in range(3):
+            top = tops_in[a, 16:24]
+            full = roll_rows(top, -4 - t)
+            after = jnp.where(zi < 7, roll_rows(roll_lanes(full, -1), 1), roll_lanes(top, t))
+            full = jnp.where(row == 0, full, after)
+            after = jnp.where(yi < 7, roll_rows(roll_lanes(full, -8), 2), roll_lanes(top, 8 * t))
+            got[a, 96:104, tile(t)] = jnp.where(row < 2, full, jnp.where(row < 4, after, zero))
+        return carry
+
+    for number in range(2):
         edges[number].wait_recv()
-    lax.fori_loop(1, NODES - 1, complete, 0)
+    steps(1, NODES - 2, NODES - 2, complete)
 
     def pair_done(pair, carry):
         start = 1 + pair * 4
@@ -549,19 +577,17 @@
 
     lax.fori_loop(0, 2, pair_done, 0)
 
-    for number in range(3, 7):
+    for number in range(2, 5):
         edges[number].wait_recv()
     complete(0, 0)
 
-    def last_plane(block, carry):
-        here = pl.ds(pl.multiple_of(block * 8, 8), 8)
+    for k in range(ROWS // 8):
+        here = slice(k * 8, k * 8 + 8)
+        end = ends_in[(k % 7) * 8 : (k % 7) * 8 + 8]
         lo = [roll_lanes(got[0, here, tile(t)], 64) for t in range(TILES)]
+        lo.append(roll_lanes(end, 64) if k < 7 else end)
         for t in range(TILES):
-            after = lo[t + 1] if t < TILES - 1 else got[9, here, tile(2)]
-            got[9, here, tile(t)] = jnp.where(low_half, lo[t], after)
-        return carry
-
-    lax.fori_loop(0, ROWS // 8, last_plane, 0)
+            got[9, here, tile(t)] = jnp.where(low_half, lo[t], lo[t + 1])
 
     for a in (0, 9):
         total = canon[c, a] + got[a]
@@ -588,7 +614,7 @@
     f32 = jnp.float32
     out = pl.pallas_call(
         kernel,
-        out_shape=jax.ShapeDtypeStruct((NODES * NODES * NODES * TILES, LANES), f32),
+        out_shape=pltpu.VMEM((NODES * NODES * NODES * TILES, LANES), f32),
         in_specs=[
             pl.BlockSpec(memory_space=pl.ANY),
             pl.BlockSpec(memory_space=pl.ANY),
@@ -613,10 +639,12 @@
             vmem((2, NODES, 16, LANES), f32),
             vmem((2, ROWS, LANES), f32),
             vmem((2, ROWS, LANES), f32),
-            vmem((NODES - 1, 16, LANES), f32),
-            vmem((NODES - 1, 16, LANES), f32),
+            vmem((NODES - 1, 24, LANES), f32),
+            vmem((NODES - 1, 24, LANES), f32),
+            vmem((56, LANES), f32),
+            vmem((56, LANES), f32),
             dma((HALF,)), dma((3, HALF)), dma((2,)), dma((2,)), dma((2, 2)), dma((2, 2)),
-            dma((NODES,)), dma((NODES,)), dma((7,)), dma((7,)),
+            dma((NODES,)), dma((NODES,)), dma((5,)), dma((5,)),
         ],
         compiler_params=pltpu.CompilerParams(
             collective_id=0, has_side_effects=True, vmem_limit_bytes=60 * 1024 * 1024

time: 57.7 us -> 45 us (0.78)
  Pallas kernels: 53.9 us -> 43.7 us
  local copies, waits for them, and re-layouts: 3.58 us -> 1.13 us
    pallas_call x1, Pallas kernels: 53.9 us -> 43.7 us  [body(): pl.pallas_call(kernel, out_shape=pltpu.VMEM((NODES * NODES * NODES * TILE...]
    unnamed x1, local copies, waits for them, and re-layouts: 3.58 us -> 1.13 us
where the time goes in v1:
time: 45 us; the launch traced here: 44.9 us
  Pallas kernels  43.7 us (97%)
  local copies, waits for them, and re-layouts  1.13 us (3%)
    pallas_call x1, Pallas kernels, body(): pl.pallas_call(kernel, out_shape=pltpu.VMEM((NODES * NODES * NODES * TILE...  43.7 us
    unnamed x1, local copies, waits for them, and re-layouts  1.13 us

profile of v1, /device:TPU:1, one launch (start us, length us, event | category | flops | bytes accessed | tf_op | source)
XLA Modules:
  0.0 44.9 jit_solution(13493516875527078760)
XLA Ops:
  0.0 43.7 %shard_map.37 = f32[3000,128]{1,0:T(8,128)S(1)} custom-call(f32[3,5,10,10,2,384]{5,4,3,2,1,0:T(2,128)} %v_hbm.1, f32[3,3,5,10,10,2,384]{6,5,4,3,2,1,0:T(2,128)} %g_hbm.1, s32[1,384]{1,0:T(1,128)} %place_ref.1), custom_call_target="tpu_custom_call" | custom-call | tf_op jit(solution)/shard_map/pallas_call | solution.py:615
  43.7 1.1 %copy.7 = f32[10,10,10,1,384]{4,3,2,1,0:T(1,128)} copy(f32[10,10,10,1,384]{4,3,2,1,0:T(1,128)S(1)} %bitcast.1) | data formatting | bytes 3072000

commit v2 on v1

--- a/solution.py
+++ b/solution.py
@@ -106,7 +106,7 @@
 
 def kernel(
     v_hbm, g_hbm, place_ref, out_ref,
-    v, g, coef, f0, fl, lhs, perm, back, place_in, canon, got,
+    v, g, coef, f0, fl, perm, back, place_in, raw, canon, got,
     zs, zr, ys, yr, xs, xr, tops, tops_in, ends, ends_in,
     v_sem, g_sem, place_sem, z_sem, y_sem, x_sem, inner_send, inner_recv, edge_send, edge_recv,
 ):
@@ -118,20 +118,35 @@
     grid_x = elem_count // GRID_Y
     sx = elem // GRID_Y
     sy = elem % GRID_Y
-    y_up = sx * GRID_Y + (sy + 1) % GRID_Y
-    y_down = sx * GRID_Y + (sy + GRID_Y - 1) % GRID_Y
-    x_up = (elem + GRID_Y) % elem_count
-    x_down = (elem + elem_count - GRID_Y) % elem_count
+    y_links = ((elem + 1, sy < GRID_Y - 1), (elem - 1, sy > 0))
+    x_links = ((elem + GRID_Y, sx < grid_x - 1), (elem - GRID_Y, sx > 0))
 
     for i in range(HALF):
         pltpu.make_async_copy(v_hbm.at[:, i], v.at[:, i], v_sem.at[i]).start()
         pltpu.make_async_copy(g_hbm.at[:, 0, i], g.at[:, 0, i], g_sem.at[0, i]).start()
-    others = (
-        (elem, o, r), (elem, c, 1 - r), (y_up, c, r), (y_down, c, r), (x_up, c, r), (x_down, c, r),
+    barrier = pltpu.get_barrier_semaphore()
+    expected = 2
+    for other in ((elem, o, r), (elem, c, 1 - r)):
+        pl.semaphore_signal(barrier, inc=1, device_id=other, device_id_type=MESH)
+    for near_elem, exists in y_links + x_links:
+        expected = expected + exists.astype(jnp.int32)
+
+        @pl.when(exists)
+        def _(near_elem=near_elem):
+            pl.semaphore_signal(barrier, inc=1, device_id=(near_elem, c, r), device_id_type=MESH)
+
+    pl.semaphore_wait(barrier, expected)
+    place_copy = pltpu.make_async_remote_copy(
+        src_ref=place_ref, dst_ref=place_in, send_sem=place_sem.at[0], recv_sem=place_sem.at[1],
+        device_id=(elem, o, r), device_id_type=MESH,
     )
-    barrier = pltpu.get_barrier_semaphore()
-    for other in others:
-        pl.semaphore_signal(barrier, inc=1, device_id=other, device_id_type=MESH)
+    place_copy.start()
+
+    for links, target in ((y_links, yr), (x_links, xr)):
+        for way in range(2):
+            @pl.when(jnp.logical_not(links[1 - way][1]))
+            def _(target=target, way=way):
+                target[way] = jnp.zeros(target.shape[1:], jnp.float32)
 
     for kind in range(2):
         for m in range(HALF):
@@ -155,14 +170,7 @@
     back[0:ELEMS, :] = back_half
     back[ELEMS : 2 * ELEMS, :] = back_half
     fill_perm(c, place_ref[...])
-    lhs[...] = jnp.zeros_like(lhs)
-
-    pl.semaphore_wait(barrier, len(others))
-    place_copy = pltpu.make_async_remote_copy(
-        src_ref=place_ref, dst_ref=place_in, send_sem=place_sem.at[0], recv_sem=place_sem.at[1],
-        device_id=(elem, o, r), device_id_type=MESH,
-    )
-    place_copy.start()
+    raw[:, :, 96:104] = jnp.zeros((2, NODES, 8, ELEMS), jnp.float32)
 
     def first_flux(i, carry):
         pltpu.make_async_copy(v_hbm.at[:, i], v.at[:, i], v_sem.at[i]).wait()
@@ -202,44 +210,58 @@
         for k in range(NODES):
             fl[b, k] = weighted([f0[i, b, k] for i in range(HALF)], weights)
 
-    def gather_rows():
-        for q in range(2):
-            for t in range(TILES):
-                for b in range(8):
-                    lhs[q, b * 8 : b * 8 + 8, tile(t)] = fl[b + 1, 1:9, q, tile(t)]
-                lhs[q, 64:72, tile(t)] = fl[1:9, 0, q, tile(t)]
-                lhs[q, 72:80, tile(t)] = fl[0, 1:9, q, tile(t)]
-                lhs[q, 80:88, tile(t)] = fl[1:9, 9, q, tile(t)]
-                lhs[q, 88:96, tile(t)] = fl[9, 1:9, q, tile(t)]
-            lhs[q, 96:97, :] = fl[0, 0, q : q + 1, :]
-            lhs[q, 97:98, :] = fl[0, 9, q : q + 1, :]
-            lhs[q, 98:99, :] = fl[9, 0, q : q + 1, :]
-            lhs[q, 99:100, :] = fl[9, 9, q : q + 1, :]
-
-    def to_canon(a):
-        for q in (o, c):
-            canon[q, a] = jnp.dot(two_parts(lhs[q]), perm[q], preferred_element_type=jnp.float32)
-
     def send_if_inner(a):
         @pl.when(is_inner(a))
         def _():
             inner_copy(a).start()
 
+    def gather_rows(a):
+        for q in range(2):
+            for t in range(TILES):
+                for b in range(8):
+                    raw[q, a, b * 8 : b * 8 + 8, tile(t)] = fl[b + 1, 1:9, q, tile(t)]
+                raw[q, a, 64:72, tile(t)] = fl[1:9, 0, q, tile(t)]
+                raw[q, a, 72:80, tile(t)] = fl[0, 1:9, q, tile(t)]
+                raw[q, a, 80:88, tile(t)] = fl[1:9, 9, q, tile(t)]
+                raw[q, a, 88:96, tile(t)] = fl[9, 1:9, q, tile(t)]
+            raw[q, a, 96:97, :] = fl[0, 0, q : q + 1, :]
+            raw[q, a, 97:98, :] = fl[0, 9, q : q + 1, :]
+            raw[q, a, 98:99, :] = fl[9, 0, q : q + 1, :]
+            raw[q, a, 99:100, :] = fl[9, 9, q : q + 1, :]
+
+    def permuted(x, matrix):
+        return jnp.dot(two_parts(x), matrix, preferred_element_type=jnp.float32)
+
+    def to_canon(a, between=None):
+        first = two_parts(raw[o, a])
+        second = two_parts(raw[c, a, 64:104])
+        if between is not None:
+            gather_rows(between)
+        canon[o, a] = jnp.dot(first, perm[o], preferred_element_type=jnp.float32)
+        canon[c, a, 64:104] = jnp.dot(second, perm[c], preferred_element_type=jnp.float32)
+        send_if_inner(a)
+
     far = HALF * o
     near = HALF * c
 
-    def far_plane(m, carry):
+    def far_plane(m):
         def at_b(b, carry):
             mix_planes(m * HALF, b)
             return carry
 
         steps(0, NODES, 2, at_b)
-        gather_rows()
-        to_canon(far + m)
-        send_if_inner(far + m)
-        return carry
-
-    lax.fori_loop(0, HALF, far_plane, 0)
+
+    def far_step(m, carry):
+        far_plane(m)
+        to_canon(far + m - 1, far + m)
+        return carry
+
+    far_plane(0)
+    gather_rows(far)
+    to_canon(far)
+    far_plane(1)
+    gather_rows(far + 1)
+    lax.fori_loop(2, HALF, far_step, 0)
 
     def near_plane(m, carry):
         for j in (1, 2):
@@ -269,12 +291,13 @@
             return carry
 
         steps(0, NODES, 2, at_k)
-        gather_rows()
-        to_canon(near + m)
-        send_if_inner(near + m)
+        to_canon(jnp.where(m == 0, far + HALF - 1, near + m - 1), near + m)
         return carry
 
     lax.fori_loop(0, HALF, near_plane, 0)
+    to_canon(near + HALF - 1)
+    for a in (0, 9):
+        canon[c, a, 0:64] = permuted(raw[c, a, 0:64], perm[c])
 
     lane = lax.broadcasted_iota(jnp.int32, (8, LANES), 1)
     row = lax.broadcasted_iota(jnp.int32, (8, LANES), 0)
@@ -288,41 +311,36 @@
     b_hi = jnp.logical_or(row == 2, row == 3)
 
     def edge_pass(step, carry):
+        planes = [2 * step, 2 * step + 1]
         spots = [
-            (q, 2 * step + k, lo_row, hi_row, tile(t))
-            for k in range(2) for q in range(2) for t in range(TILES) for lo_row, hi_row in ((64, 80), (72, 88))
+            (q, a, lo_row, hi_row, tile(t))
+            for a in planes for q in range(2) for t in range(TILES) for lo_row, hi_row in ((64, 80), (72, 88))
         ]
+        corner_spots = [(q, a, tile(t)) for a in planes for q in range(2) for t in range(TILES)]
+        corners = [canon[q, a, 96:104, lanes] for q, a, lanes in corner_spots]
         held = [
             (canon[q, a, lo_row : lo_row + 8, lanes], canon[q, a, hi_row : hi_row + 8, lanes])
             for q, a, lo_row, hi_row, lanes in spots
+        ]
+        corners = [
+            k
+            + jnp.where(jnp.logical_and(c_lo, zi > 0), roll_lanes(roll_rows(k, -1), 1), zero)
+            + jnp.where(jnp.logical_and(c_hi, zi < 7), roll_lanes(roll_rows(k, 1), -1), zero)
+            for k in corners
         ]
         for (q, a, lo_row, hi_row, lanes), (lo, hi) in zip(spots, held):
             index, shift = (zi, 1) if lo_row == 64 else (yi, 8)
             canon[q, a, lo_row : lo_row + 8, lanes] = lo + jnp.where(index > 0, roll_lanes(hi, shift), zero)
             canon[q, a, hi_row : hi_row + 8, lanes] = hi + jnp.where(index < 7, roll_lanes(lo, -shift), zero)
-        return carry
-
-    def corner_pass(step, carry):
-        spots = [(q, 5 * step + k, tile(t)) for k in range(5) for q in range(2) for t in range(TILES)]
-        held = [canon[q, a, 96:104, lanes] for q, a, lanes in spots]
-        held = [
-            k
-            + jnp.where(jnp.logical_and(c_lo, zi > 0), roll_lanes(roll_rows(k, -1), 1), zero)
-            + jnp.where(jnp.logical_and(c_hi, zi < 7), roll_lanes(roll_rows(k, 1), -1), zero)
-            for k in held
-        ]
-        held = [
-            k
-            + jnp.where(jnp.logical_and(b_lo, yi > 0), roll_lanes(roll_rows(k, -2), 8), zero)
-            + jnp.where(jnp.logical_and(b_hi, yi < 7), roll_lanes(roll_rows(k, 2), -8), zero)
-            for k in held
-        ]
-        for (q, a, lanes), k in zip(spots, held):
-            canon[q, a, 96:104, lanes] = k
+        for (q, a, lanes), k in zip(corner_spots, corners):
+            canon[q, a, 96:104, lanes] = (
+                k
+                + jnp.where(jnp.logical_and(b_lo, yi > 0), roll_lanes(roll_rows(k, -2), 8), zero)
+                + jnp.where(jnp.logical_and(b_hi, yi < 7), roll_lanes(roll_rows(k, 2), -8), zero)
+            )
         return carry
 
     lax.fori_loop(0, NODES // 2, edge_pass, 0)
-    lax.fori_loop(0, 2, corner_pass, 0)
 
     def x_pass(block, carry):
         here = pl.ds(block * 8, 8)
@@ -393,8 +411,7 @@
         @pl.when(is_inner(a))
         def _():
             inner_copy(a).wait_recv()
-            total = canon[c, a, 0:64] + got[a, 0:64]
-            value = jnp.dot(two_parts(total), back[...], preferred_element_type=jnp.float32)
+            value = permuted(got[a, 0:64], back[...]) + raw[c, a, 0:64]
             for t in range(TILES):
                 for b in range(8):
                     put(a, b + 1, value, t, b * 8)
@@ -441,22 +458,27 @@
     y_copies = [
         pltpu.make_async_remote_copy(
             src_ref=ys.at[way], dst_ref=yr.at[way], send_sem=y_sem.at[0, way], recv_sem=y_sem.at[1, way],
-            device_id=(y_up if way == 0 else y_down, c, r), device_id_type=MESH,
+            device_id=(y_links[way][0], c, r), device_id_type=MESH,
         )
         for way in range(2)
     ]
-    for copy in y_copies:
-        copy.start()
+    for way in range(2):
+        @pl.when(y_links[way][1])
+        def _(copy=y_copies[way]):
+            copy.start()
+
 
     lax.fori_loop(near + 2, near + 4, inner_done, 0)
 
-    for copy in y_copies:
-        copy.wait_recv()
-    y_has_up, y_has_down = on(sy < GRID_Y - 1), on(sy > 0)
+    for way in range(2):
+        @pl.when(y_links[1 - way][1])
+        def _(copy=y_copies[way]):
+            copy.wait_recv()
+
 
     def y_unpack(a, carry):
-        below = [yr[0, a, 0:8] * y_has_down, roll_rows(yr[0, a, 8:16], -2) * y_has_down]
-        above = [yr[1, a, 0:8] * y_has_up, roll_rows(yr[1, a, 8:16], 2) * y_has_up]
+        below = [yr[0, a, 0:8], roll_rows(yr[0, a, 8:16], -2)]
+        above = [yr[1, a, 0:8], roll_rows(yr[1, a, 8:16], 2)]
         for q in range(2):
             for t in range(TILES):
                 u = 3 * q + t
@@ -483,12 +505,15 @@
     x_copies = [
         pltpu.make_async_remote_copy(
             src_ref=xs.at[way], dst_ref=xr.at[way], send_sem=x_sem.at[0, way], recv_sem=x_sem.at[1, way],
-            device_id=(x_up if way == 0 else x_down, c, r), device_id_type=MESH,
+            device_id=(x_links[way][0], c, r), device_id_type=MESH,
         )
         for way in range(2)
     ]
-    for copy in x_copies:
-        copy.start()
+    for way in range(2):
+        @pl.when(x_links[way][1])
+        def _(copy=x_copies[way]):
+            copy.start()
+
 
     def edge_copy(number, source, target):
         return pltpu.make_async_remote_copy(
@@ -505,13 +530,14 @@
     ]
 
     def fill_tops(a, carry):
-        tops[a, 0:8] = pack_top([canon[o, a, 80:88, tile(t)] for t in range(TILES)], zi, 1)
-        tops[a, 8:16] = pack_top([canon[o, a, 88:96, tile(t)] for t in range(TILES)], yi, 8)
+        z_top = pack_top([canon[o, a, 80:88, tile(t)] for t in range(TILES)], zi, 1)
+        y_top = pack_top([canon[o, a, 88:96, tile(t)] for t in range(TILES)], yi, 8)
+        tops[a, 0:8] = jnp.where(yi > 4, y_top, jnp.where(zi > 4, z_top, roll_lanes(z_top, -27)))
         corner = [canon[o, a, 96:104, tile(t)] for t in range(TILES)]
         packed = jnp.where(row < 2, pack_top(corner, zi, 1), pack_top(corner, yi, 8))
         for t in range(TILES):
             packed = jnp.where(row == 4 + t, roll_rows(corner[t], 4 + t), packed)
-        tops[a, 16:24] = packed
+        tops[a, 8:16] = packed
         return carry
 
     edges[0].start()
@@ -519,14 +545,16 @@
     lax.fori_loop(near + 4, near + 5, inner_done, 0)
     edges[1].start()
 
-    for copy in x_copies:
-        copy.wait_recv()
-    x_has_up, x_has_down = on(sx < grid_x - 1), on(sx > 0)
+    for way in range(2):
+        @pl.when(x_links[1 - way][1])
+        def _(copy=x_copies[way]):
+            copy.wait_recv()
+
 
     def x_unpack(block, carry):
         here = pl.ds(block * 8, 8)
-        below = xr[0, here] * x_has_down
-        above = xr[1, here] * x_has_up
+        below = xr[0, here]
+        above = xr[1, here]
         low = (jnp.where(low_half, below, zero), jnp.where(low_half, roll_lanes(below, 64), zero))
         top = (jnp.where(low_half, zero, roll_lanes(above, 64)), jnp.where(low_half, zero, above))
         for q in range(2):
@@ -549,11 +577,11 @@
         for t in range(TILES):
             top = tops_in[a, 0:8]
             lo = got[a, 64:72, tile(t)]
-            got[a, 80:88, tile(t)] = jnp.where(zi < 7, roll_lanes(lo, -1), roll_lanes(top, t))
-            top = tops_in[a, 8:16]
+            z_top = jnp.where(yi < 5, roll_lanes(top, t), roll_lanes(top, 27 + t))
+            got[a, 80:88, tile(t)] = jnp.where(zi < 7, roll_lanes(lo, -1), z_top)
             lo = got[a, 72:80, tile(t)]
             got[a, 88:96, tile(t)] = jnp.where(yi < 7, roll_lanes(lo, -8), roll_lanes(top, 8 * t))
-            top = tops_in[a, 16:24]
+            top = tops_in[a, 8:16]
             full = roll_rows(top, -4 - t)
             after = jnp.where(zi < 7, roll_rows(roll_lanes(full, -1), 1), roll_lanes(top, t))
             full = jnp.where(row == 0, full, after)
@@ -568,9 +596,7 @@
     def pair_done(pair, carry):
         start = 1 + pair * 4
         total = canon[c, pl.ds(start, 4), 64:104] + got[pl.ds(start, 4), 64:104]
-        value = jnp.dot(
-            two_parts(total.reshape(160, ELEMS)), back[...], preferred_element_type=jnp.float32
-        )
+        value = permuted(total.reshape(160, ELEMS), back[...])
         for k in range(4):
             put_edges(start + k, value, k * 40)
         return carry
@@ -591,15 +617,20 @@
 
     for a in (0, 9):
         total = canon[c, a] + got[a]
-        value = jnp.dot(two_parts(total), back[...], preferred_element_type=jnp.float32)
+        value = permuted(total, back[...])
         for t in range(TILES):
             for b in range(8):
                 put(a, b + 1, value, t, b * 8)
         put_edges(a, value, 64)
 
     z_copy.wait_send()
-    for copy in y_copies + x_copies + edges:
+    for copy in edges:
         copy.wait_send()
+    for links, copies in ((y_links, y_copies), (x_links, x_copies)):
+        for way in range(2):
+            @pl.when(links[way][1])
+            def _(copy=copies[way]):
+                copy.wait_send()
 
     def sent(a, carry):
         inner_copy(a).wait_send()
@@ -627,10 +658,10 @@
             pltpu.SMEM((2 * HALF * HALF,), f32),
             vmem((HALF, NODES, NODES, 2, ELEMS), f32),
             vmem((NODES, NODES, 2, ELEMS), f32),
-            vmem((2, ROWS, ELEMS), f32),
             vmem((2, 2 * ELEMS, ELEMS), jnp.bfloat16),
             vmem((2 * ELEMS, ELEMS), jnp.bfloat16),
             vmem((1, ELEMS), jnp.int32),
+            vmem((2, NODES, ROWS, ELEMS), f32),
             vmem((2, NODES, ROWS, ELEMS), f32),
             vmem((NODES, ROWS, ELEMS), f32),
             vmem((2, NODES, 16, LANES), f32),
@@ -639,8 +670,8 @@
             vmem((2, NODES, 16, LANES), f32),
             vmem((2, ROWS, LANES), f32),
             vmem((2, ROWS, LANES), f32),
-            vmem((NODES - 1, 24, LANES), f32),
-            vmem((NODES - 1, 24, LANES), f32),
+            vmem((NODES - 1, 16, LANES), f32),
+            vmem((NODES - 1, 16, LANES), f32),
             vmem((56, LANES), f32),
             vmem((56, LANES), f32),
             dma((HALF,)), dma((3, HALF)), dma((2,)), dma((2,)), dma((2, 2)), dma((2, 2)),

time: 45 us -> 39.8 us (0.88)
  the two profiles are of different devices: /device:TPU:1 before, /device:TPU:39 now
where the time goes in v2:
time: 39.8 us; the launch traced here: 39.7 us
  Pallas kernels  38.5 us (97%)
  local copies, waits for them, and re-layouts  1.13 us (3%)
    pallas_call x1, Pallas kernels, body(): pl.pallas_call(kernel, out_shape=pltpu.VMEM((NODES * NODES * NODES * TILE...  38.5 us
    unnamed x1, local copies, waits for them, and re-layouts  1.13 us

profile of v2, /device:TPU:39, one launch (start us, length us, event | category | flops | bytes accessed | tf_op | source)
XLA Modules:
  0.0 39.7 jit_solution(8811090858984072482)
XLA Ops:
  0.0 38.5 %shard_map.37 = f32[3000,128]{1,0:T(8,128)S(1)} custom-call(f32[3,5,10,10,2,384]{5,4,3,2,1,0:T(2,128)} %v_hbm.1, f32[3,3,5,10,10,2,384]{6,5,4,3,2,1,0:T(2,128)} %g_hbm.1, s32[1,384]{1,0:T(1,128)} %place_ref.1), custom_call_target="tpu_custom_call" | custom-call | tf_op jit(solution)/shard_map/pallas_call | solution.py:646
  38.5 1.1 %copy.7 = f32[10,10,10,1,384]{4,3,2,1,0:T(1,128)} copy(f32[10,10,10,1,384]{4,3,2,1,0:T(1,128)S(1)} %bitcast.1) | data formatting | bytes 3072000

commit v3 on v2

--- a/solution.py
+++ b/solution.py
@@ -106,9 +106,9 @@
 
 def kernel(
     v_hbm, g_hbm, place_ref, out_ref,
-    v, g, coef, f0, fl, perm, back, place_in, raw, canon, got,
+    v, g, coef, f0, fl, fn, perm, back, place_in, raw, canon, got,
     zs, zr, ys, yr, xs, xr, tops, tops_in, ends, ends_in,
-    v_sem, g_sem, place_sem, z_sem, y_sem, x_sem, inner_send, inner_recv, edge_send, edge_recv,
+    first_sem, later_sem, place_sem, z_sem, y_sem, x_sem, send_sem, inner_sem, edge_sem,
 ):
     elem = lax.axis_index("elem")
     c = lax.axis_index("comp")
@@ -121,9 +121,24 @@
     y_links = ((elem + 1, sy < GRID_Y - 1), (elem - 1, sy > 0))
     x_links = ((elem + GRID_Y, sx < grid_x - 1), (elem - GRID_Y, sx > 0))
 
+    def first_copies(i, half):
+        here = slice(half * HALF, half * HALF + HALF)
+        return (
+            pltpu.make_async_copy(v_hbm.at[:, i, here], v.at[:, i, here], first_sem.at[half, i]),
+            pltpu.make_async_copy(g_hbm.at[:, 0, i, here], g.at[:, 0, i, here], first_sem.at[half, i]),
+        )
+
+    def first_arrived(i, half):
+        here = slice(half * HALF, half * HALF + HALF)
+        pltpu.make_async_copy(g_hbm.at[:, 0:2, i, here], g.at[:, 0:2, i, here], first_sem.at[half, i]).wait()
+
+    def later_copy(i):
+        return pltpu.make_async_copy(g_hbm.at[:, 1:3, i], g.at[:, 1:3, i], later_sem.at[i])
+
     for i in range(HALF):
-        pltpu.make_async_copy(v_hbm.at[:, i], v.at[:, i], v_sem.at[i]).start()
-        pltpu.make_async_copy(g_hbm.at[:, 0, i], g.at[:, 0, i], g_sem.at[0, i]).start()
+        for copy in first_copies(i, 0):
+            copy.start()
+
     barrier = pltpu.get_barrier_semaphore()
     expected = 2
     for other in ((elem, o, r), (elem, c, 1 - r)):
@@ -172,100 +187,100 @@
     fill_perm(c, place_ref[...])
     raw[:, :, 96:104] = jnp.zeros((2, NODES, 8, ELEMS), jnp.float32)
 
-    def first_flux(i, carry):
-        pltpu.make_async_copy(v_hbm.at[:, i], v.at[:, i], v_sem.at[i]).wait()
-        pltpu.make_async_copy(g_hbm.at[:, 0, i], g.at[:, 0, i], g_sem.at[0, i]).wait()
-        for j in (1, 2):
-            pltpu.make_async_copy(g_hbm.at[:, j, i], g.at[:, j, i], g_sem.at[j, i]).start()
-
-        def at_b(b, carry):
+    far = HALF * o
+    near = HALF * c
+
+    def inner_copy(a, rows):
+        return pltpu.make_async_remote_copy(
+            src_ref=raw.at[o, a, rows], dst_ref=got.at[a, rows], send_sem=send_sem.at[0], recv_sem=inner_sem.at[a - 1],
+            device_id=(elem, o, r), device_id_type=MESH,
+        )
+
+    def is_inner(a):
+        return jnp.logical_and(a > 0, a < NODES - 1)
+
+    def send_inner(a, halves):
+        @pl.when(is_inner(a))
+        def _():
+            for half in halves:
+                inner_copy(a, slice(half * 32, half * 32 + 32)).start()
+
+    def first_flux(half):
+        def at_plane(i, carry):
+            first_arrived(i, half)
+            for copy in first_copies(i, 1) if half == 0 else (later_copy(i),):
+                copy.start()
+
+            def at_b(b, carry):
+                for k in range(NODES):
+                    f0[i, b, k] = (
+                        g[0, 0, i, b, k] * v[0, i, b, k]
+                        + g[1, 0, i, b, k] * v[1, i, b, k]
+                        + g[2, 0, i, b, k] * v[2, i, b, k]
+                    )
+
+            for b in range(half * HALF, half * HALF + HALF):
+                at_b(b, 0)
+            return carry
+
+        return at_plane
+
+    def mix_planes(m, half):
+        weights = [coef[m * HALF + i] for i in range(HALF)]
+        for b in range(half * HALF, half * HALF + HALF):
             for k in range(NODES):
-                f0[i, b, k] = (
-                    g[0, 0, i, b, k] * v[0, i, b, k]
-                    + g[1, 0, i, b, k] * v[1, i, b, k]
-                    + g[2, 0, i, b, k] * v[2, i, b, k]
-                )
-            return carry
-
-        steps(0, NODES, 2, at_b)
-        return carry
-
-    lax.fori_loop(0, HALF, first_flux, 0)
-
+                fl[m, b, k] = weighted([f0[i, b, k] for i in range(HALF)], weights)
+
+    def gather_inner(m, a, half):
+        for q in range(2):
+            for t in range(TILES):
+                for b in range(half * 4, half * 4 + 4):
+                    raw[q, a, b * 8 : b * 8 + 8, tile(t)] = fl[m, b + 1, 1:9, q, tile(t)]
+
+    def gather_edges(m, a):
+        for q in range(2):
+            for t in range(TILES):
+                raw[q, a, 64:72, tile(t)] = fl[m, 1:9, 0, q, tile(t)]
+                raw[q, a, 72:80, tile(t)] = fl[m, 0, 1:9, q, tile(t)]
+                raw[q, a, 80:88, tile(t)] = fl[m, 1:9, 9, q, tile(t)]
+                raw[q, a, 88:96, tile(t)] = fl[m, 9, 1:9, q, tile(t)]
+            raw[q, a, 96:97, :] = fl[m, 0, 0, q : q + 1, :]
+            raw[q, a, 97:98, :] = fl[m, 0, 9, q : q + 1, :]
+            raw[q, a, 98:99, :] = fl[m, 9, 0, q : q + 1, :]
+            raw[q, a, 99:100, :] = fl[m, 9, 9, q : q + 1, :]
+
+    def permuted(x, matrix):
+        return jnp.dot(two_parts(x), matrix, preferred_element_type=jnp.float32)
+
+    def to_canon(a, between=None):
+        parts = [two_parts(raw[q, a, 64:104]) for q in range(2)]
+        if between is not None:
+            between()
+        for q in range(2):
+            canon[q, a, 64:104] = jnp.dot(parts[q], perm[q], preferred_element_type=jnp.float32)
+
+    def far_first(m, carry):
+        mix_planes(m, 0)
+        gather_inner(m, far + m, 0)
+        send_inner(far + m, (0,))
+        return carry
+
+    def far_second(m, carry):
+        mix_planes(m, 1)
+        gather_inner(m, far + m, 1)
+        send_inner(far + m, (1,))
+        gather_edges(m, far + m)
+        return carry
+
+    lax.fori_loop(0, HALF, first_flux(0), 0)
+    lax.fori_loop(0, HALF, far_first, 0)
+    lax.fori_loop(0, HALF, first_flux(1), 0)
+    lax.fori_loop(0, HALF, far_second, 0)
     place_copy.wait()
     fill_perm(o, place_in[...])
 
-    def inner_copy(a):
-        return pltpu.make_async_remote_copy(
-            src_ref=canon.at[o, a, 0:64], dst_ref=got.at[a, 0:64],
-            send_sem=inner_send.at[a], recv_sem=inner_recv.at[a],
-            device_id=(elem, o, r), device_id_type=MESH,
-        )
-
-    def is_inner(a):
-        return jnp.logical_and(a > 0, a < NODES - 1)
-
-    def mix_planes(base, b):
-        weights = [coef[base + i] for i in range(HALF)]
-        for k in range(NODES):
-            fl[b, k] = weighted([f0[i, b, k] for i in range(HALF)], weights)
-
-    def send_if_inner(a):
-        @pl.when(is_inner(a))
-        def _():
-            inner_copy(a).start()
-
-    def gather_rows(a):
-        for q in range(2):
-            for t in range(TILES):
-                for b in range(8):
-                    raw[q, a, b * 8 : b * 8 + 8, tile(t)] = fl[b + 1, 1:9, q, tile(t)]
-                raw[q, a, 64:72, tile(t)] = fl[1:9, 0, q, tile(t)]
-                raw[q, a, 72:80, tile(t)] = fl[0, 1:9, q, tile(t)]
-                raw[q, a, 80:88, tile(t)] = fl[1:9, 9, q, tile(t)]
-                raw[q, a, 88:96, tile(t)] = fl[9, 1:9, q, tile(t)]
-            raw[q, a, 96:97, :] = fl[0, 0, q : q + 1, :]
-            raw[q, a, 97:98, :] = fl[0, 9, q : q + 1, :]
-            raw[q, a, 98:99, :] = fl[9, 0, q : q + 1, :]
-            raw[q, a, 99:100, :] = fl[9, 9, q : q + 1, :]
-
-    def permuted(x, matrix):
-        return jnp.dot(two_parts(x), matrix, preferred_element_type=jnp.float32)
-
-    def to_canon(a, between=None):
-        first = two_parts(raw[o, a])
-        second = two_parts(raw[c, a, 64:104])
-        if between is not None:
-            gather_rows(between)
-        canon[o, a] = jnp.dot(first, perm[o], preferred_element_type=jnp.float32)
-        canon[c, a, 64:104] = jnp.dot(second, perm[c], preferred_element_type=jnp.float32)
-        send_if_inner(a)
-
-    far = HALF * o
-    near = HALF * c
-
-    def far_plane(m):
-        def at_b(b, carry):
-            mix_planes(m * HALF, b)
-            return carry
-
-        steps(0, NODES, 2, at_b)
-
-    def far_step(m, carry):
-        far_plane(m)
-        to_canon(far + m - 1, far + m)
-        return carry
-
-    far_plane(0)
-    gather_rows(far)
-    to_canon(far)
-    far_plane(1)
-    gather_rows(far + 1)
-    lax.fori_loop(2, HALF, far_step, 0)
-
     def near_plane(m, carry):
-        for j in (1, 2):
-            pltpu.make_async_copy(g_hbm.at[:, j, m], g.at[:, j, m], g_sem.at[j, m]).wait()
+        later_copy(m).wait()
 
         def flux(j, b, k):
             return (
@@ -279,7 +294,7 @@
             weights = [coef[base + i] for i in range(HALF)]
             out = along([flux(2, b, k) for k in range(NODES)])
             for k in range(NODES):
-                fl[b, k] = out[k] + weighted([f0[i, b, k] for i in range(HALF)], weights)
+                fn[b, k] = out[k] + weighted([f0[i, b, k] for i in range(HALF)], weights)
             return carry
 
         steps(0, NODES, 2, at_b)
@@ -287,17 +302,30 @@
         def at_k(k, carry):
             out = along([flux(1, b, k) for b in range(NODES)])
             for b in range(NODES):
-                fl[b, k] = fl[b, k] + out[b]
+                fl[m, b, k] = fn[b, k] + out[b]
             return carry
 
         steps(0, NODES, 2, at_k)
-        to_canon(jnp.where(m == 0, far + HALF - 1, near + m - 1), near + m)
+
+        def between():
+            gather_inner(m, near + m, 0)
+            gather_inner(m, near + m, 1)
+            gather_edges(m, near + m)
+
+        to_canon(far + m, between)
+
+        @pl.when(m < 3 - c)
+        def _():
+            send_inner(near + m, (0, 1))
+
         return carry
 
     lax.fori_loop(0, HALF, near_plane, 0)
-    to_canon(near + HALF - 1)
-    for a in (0, 9):
-        canon[c, a, 0:64] = permuted(raw[c, a, 0:64], perm[c])
+
+    for q in range(2):
+        canon[q, pl.ds(near, HALF), 64:104] = permuted(
+            raw[q, pl.ds(near, HALF), 64:104].reshape(HALF * 40, ELEMS), perm[q]
+        ).reshape(HALF, 40, ELEMS)
 
     lane = lax.broadcasted_iota(jnp.int32, (8, LANES), 1)
     row = lax.broadcasted_iota(jnp.int32, (8, LANES), 0)
@@ -310,37 +338,32 @@
     b_lo = row < 2
     b_hi = jnp.logical_or(row == 2, row == 3)
 
-    def edge_pass(step, carry):
-        planes = [2 * step, 2 * step + 1]
-        spots = [
-            (q, a, lo_row, hi_row, tile(t))
-            for a in planes for q in range(2) for t in range(TILES) for lo_row, hi_row in ((64, 80), (72, 88))
-        ]
-        corner_spots = [(q, a, tile(t)) for a in planes for q in range(2) for t in range(TILES)]
-        corners = [canon[q, a, 96:104, lanes] for q, a, lanes in corner_spots]
-        held = [
-            (canon[q, a, lo_row : lo_row + 8, lanes], canon[q, a, hi_row : hi_row + 8, lanes])
-            for q, a, lo_row, hi_row, lanes in spots
-        ]
-        corners = [
-            k
-            + jnp.where(jnp.logical_and(c_lo, zi > 0), roll_lanes(roll_rows(k, -1), 1), zero)
-            + jnp.where(jnp.logical_and(c_hi, zi < 7), roll_lanes(roll_rows(k, 1), -1), zero)
-            for k in corners
-        ]
-        for (q, a, lo_row, hi_row, lanes), (lo, hi) in zip(spots, held):
-            index, shift = (zi, 1) if lo_row == 64 else (yi, 8)
-            canon[q, a, lo_row : lo_row + 8, lanes] = lo + jnp.where(index > 0, roll_lanes(hi, shift), zero)
-            canon[q, a, hi_row : hi_row + 8, lanes] = hi + jnp.where(index < 7, roll_lanes(lo, -shift), zero)
-        for (q, a, lanes), k in zip(corner_spots, corners):
-            canon[q, a, 96:104, lanes] = (
-                k
-                + jnp.where(jnp.logical_and(b_lo, yi > 0), roll_lanes(roll_rows(k, -2), 8), zero)
-                + jnp.where(jnp.logical_and(b_hi, yi < 7), roll_lanes(roll_rows(k, 2), -8), zero)
-            )
-        return carry
-
-    lax.fori_loop(0, NODES // 2, edge_pass, 0)
+    def line_pass(lo_row, index, shift, corner_lo, corner_hi, corner_step):
+        def two_planes(step, carry):
+            spots = [(q, 2 * step + k, tile(t)) for k in range(2) for q in range(2) for t in range(TILES)]
+            corners = [canon[q, a, 96:104, lanes] for q, a, lanes in spots]
+            lows = [canon[q, a, lo_row : lo_row + 8, lanes] for q, a, lanes in spots]
+            highs = [canon[q, a, lo_row + 16 : lo_row + 24, lanes] for q, a, lanes in spots]
+            for (q, a, lanes), k, lo, hi in zip(spots, corners, lows, highs):
+                canon[q, a, lo_row : lo_row + 8, lanes] = lo + jnp.where(index > 0, roll_lanes(hi, shift), zero)
+                canon[q, a, lo_row + 16 : lo_row + 24, lanes] = hi + jnp.where(
+                    index < 7, roll_lanes(lo, -shift), zero
+                )
+                canon[q, a, 96:104, lanes] = (
+                    k
+                    + jnp.where(
+                        jnp.logical_and(corner_lo, index > 0), roll_lanes(roll_rows(k, -corner_step), shift), zero
+                    )
+                    + jnp.where(
+                        jnp.logical_and(corner_hi, index < 7), roll_lanes(roll_rows(k, corner_step), -shift), zero
+                    )
+                )
+            return carry
+
+        return two_planes
+
+    z_pass = line_pass(64, zi, 1, c_lo, c_hi, 1)
+    y_pass = line_pass(72, yi, 8, b_lo, b_hi, 2)
 
     def x_pass(block, carry):
         here = pl.ds(block * 8, 8)
@@ -354,8 +377,6 @@
                 canon[q, 9, here, tile(t)] = hi[t] + jnp.where(low_half, lo_rolled[t], lo_rolled[t + 1])
         return carry
 
-    steps(0, ROWS // 8, 13, x_pass)
-
     def pack_top(parts, index, step):
         total = parts[0]
         for u in range(1, len(parts)):
@@ -388,6 +409,43 @@
         device_id=(elem, c, 1 - r), device_id_type=MESH,
     )
     z_copy.start()
+
+    def x_pack(block, carry):
+        here = pl.ds(block * 8, 8)
+        xs[0, here] = jnp.where(low_half, roll_lanes(canon[0, 9, here, tile(2)], 64), canon[1, 9, here, tile(2)])
+        xs[1, here] = jnp.where(low_half, canon[0, 0, here, tile(0)], roll_lanes(canon[1, 0, here, tile(0)], 64))
+        return carry
+
+    def x_copy(part, way):
+        rows = slice(0, 64) if part == 0 else slice(64, ROWS)
+        return pltpu.make_async_remote_copy(
+            src_ref=xs.at[way, rows], dst_ref=xr.at[way, rows],
+            send_sem=x_sem.at[0, part, way], recv_sem=x_sem.at[1, part, way],
+            device_id=(x_links[way][0], c, r), device_id_type=MESH,
+        )
+
+    def x_send(part):
+        for way in range(2):
+            @pl.when(x_links[way][1])
+            def _(copy=x_copy(part, way)):
+                copy.start()
+
+    def x_wait(part):
+        for way in range(2):
+            @pl.when(x_links[1 - way][1])
+            def _(copy=x_copy(part, way)):
+                copy.wait_recv()
+
+    def x_unpack(block, carry):
+        here = pl.ds(block * 8, 8)
+        below = xr[0, here]
+        above = xr[1, here]
+        low = (jnp.where(low_half, below, zero), jnp.where(low_half, roll_lanes(below, 64), zero))
+        top = (jnp.where(low_half, zero, roll_lanes(above, 64)), jnp.where(low_half, zero, above))
+        for q in range(2):
+            canon[q, 0, here, tile(0)] = canon[q, 0, here, tile(0)] + low[q]
+            canon[q, 9, here, tile(2)] = canon[q, 9, here, tile(2)] + top[q]
+        return carry
 
     def put(a, b_row, value, t, first):
         start = ((a * 10 + b_row) * 10 + 1) * 3 + t
@@ -410,15 +468,46 @@
     def inner_done(a, carry):
         @pl.when(is_inner(a))
         def _():
-            inner_copy(a).wait_recv()
-            value = permuted(got[a, 0:64], back[...]) + raw[c, a, 0:64]
+            inner_copy(a, slice(0, 64)).wait_recv()
             for t in range(TILES):
+                value = got[a, 0:64, tile(t)] + raw[c, a, 0:64, tile(t)]
                 for b in range(8):
-                    put(a, b + 1, value, t, b * 8)
-
-        return carry
-
-    lax.fori_loop(near, near + 2, inner_done, 0)
+                    start = ((a * 10 + b + 1) * 10 + 1) * 3 + t
+                    out_ref[pl.ds(start, 8, stride=3), :] = value[b * 8 : b * 8 + 8]
+
+        return carry
+
+    for q in range(2):
+        both = jnp.concatenate([raw[q, 0, 0:64], raw[q, 9, 0:64]], axis=0)
+        both = permuted(both, perm[q])
+        canon[q, 0, 0:64] = both[0:64]
+        canon[q, 9, 0:64] = both[64:128]
+    steps(0, 8, 8, x_pack)
+    x_send(0)
+
+    def send_late(a, carry):
+        send_inner(a, (0, 1))
+        return carry
+
+    lax.fori_loop(near + 3 - c, near + HALF, send_late, 0)
+    lax.fori_loop(0, NODES // 2, z_pass, 0)
+    def edge_copy(group, source, target):
+        return pltpu.make_async_remote_copy(
+            src_ref=source, dst_ref=target, send_sem=send_sem.at[group + 1], recv_sem=edge_sem.at[group],
+            device_id=(elem, o, r), device_id_type=MESH,
+        )
+
+    z_rows = edge_copy(0, canon.at[o, 1:9, 64:72], got.at[1:9, 64:72])
+    y_rows = edge_copy(0, canon.at[o, 1:9, 72:80], got.at[1:9, 72:80])
+    most_tops = edge_copy(0, tops.at[1:9], tops_in.at[1:9])
+    x_inner = edge_copy(1, canon.at[o, 0, 0:64], got.at[0, 0:64])
+    x_edges = edge_copy(1, canon.at[o, 0, 64:80], got.at[0, 64:80])
+    x_tops = edge_copy(1, tops.at[0], tops_in.at[0])
+    x_ends = edge_copy(1, ends, ends_in)
+    whole_groups = (
+        edge_copy(0, canon.at[o, 1:9, 0:64, 0:LANES], got.at[1:9, 0:64, 0:LANES]),
+        edge_copy(1, canon.at[o, 9], got.at[9]),
+    )
 
     z_copy.wait_recv()
     r0, r1 = on(r == 0), on(r == 1)
@@ -446,15 +535,20 @@
 
     steps(0, NODES, NODES, z_unpack)
 
-    def y_pack(a, carry):
-        corner = six(a, slice(96, 104))
-        ys[0, a, 0:8] = pack_top(six(a, slice(88, 96)), yi, 8)
-        ys[0, a, 8:16] = pack_top(corner, yi, 8)
-        ys[1, a, 0:8] = pack_low(six(a, slice(72, 80)), yi, 8)
-        ys[1, a, 8:16] = pack_low(corner, yi, 8)
-        return carry
-
-    steps(0, NODES, NODES, y_pack)
+    z_rows.start()
+
+    for a in range(NODES):
+        ys[0, a * 8 : a * 8 + 8] = pack_top(six(a, slice(88, 96)), yi, 8)
+        ys[1, a * 8 : a * 8 + 8] = pack_low(six(a, slice(72, 80)), yi, 8)
+    for group in range(3):
+        top_total, low_total = zero, zero
+        for k, a in enumerate(range(4 * group, min(4 * group + 4, NODES))):
+            corner = six(a, slice(96, 104))
+            mine = row // 2 == k
+            top_total = jnp.where(mine, roll_rows(pack_top(corner, yi, 8), 2 * k - 2), top_total)
+            low_total = jnp.where(mine, roll_rows(pack_low(corner, yi, 8), 2 * k), low_total)
+        ys[0, 80 + group * 8 : 88 + group * 8] = top_total
+        ys[1, 80 + group * 8 : 88 + group * 8] = low_total
     y_copies = [
         pltpu.make_async_remote_copy(
             src_ref=ys.at[way], dst_ref=yr.at[way], send_sem=y_sem.at[0, way], recv_sem=y_sem.at[1, way],
@@ -468,8 +562,9 @@
             copy.start()
 
 
-    lax.fori_loop(near + 2, near + 4, inner_done, 0)
-
+    lax.fori_loop(0, NODES // 2, y_pass, 0)
+    steps(0, 8, 8, x_pass)
+    lax.fori_loop(near, near + 2, inner_done, 0)
     for way in range(2):
         @pl.when(y_links[1 - way][1])
         def _(copy=y_copies[way]):
@@ -477,8 +572,9 @@
 
 
     def y_unpack(a, carry):
-        below = [yr[0, a, 0:8], roll_rows(yr[0, a, 8:16], -2)]
-        above = [yr[1, a, 0:8], roll_rows(yr[1, a, 8:16], 2)]
+        group, k = 80 + a // 4 * 8, a % 4
+        below = [yr[0, a * 8 : a * 8 + 8], roll_rows(yr[0, group : group + 8], -2 * k)]
+        above = [yr[1, a * 8 : a * 8 + 8], roll_rows(yr[1, group : group + 8], 2 - 2 * k)]
         for q in range(2):
             for t in range(TILES):
                 u = 3 * q + t
@@ -495,40 +591,6 @@
 
     steps(0, NODES, NODES, y_unpack)
 
-    def x_pack(block, carry):
-        here = pl.ds(block * 8, 8)
-        xs[0, here] = jnp.where(low_half, roll_lanes(canon[0, 9, here, tile(2)], 64), canon[1, 9, here, tile(2)])
-        xs[1, here] = jnp.where(low_half, canon[0, 0, here, tile(0)], roll_lanes(canon[1, 0, here, tile(0)], 64))
-        return carry
-
-    steps(0, ROWS // 8, 13, x_pack)
-    x_copies = [
-        pltpu.make_async_remote_copy(
-            src_ref=xs.at[way], dst_ref=xr.at[way], send_sem=x_sem.at[0, way], recv_sem=x_sem.at[1, way],
-            device_id=(x_links[way][0], c, r), device_id_type=MESH,
-        )
-        for way in range(2)
-    ]
-    for way in range(2):
-        @pl.when(x_links[way][1])
-        def _(copy=x_copies[way]):
-            copy.start()
-
-
-    def edge_copy(number, source, target):
-        return pltpu.make_async_remote_copy(
-            src_ref=source, dst_ref=target, send_sem=edge_send.at[number], recv_sem=edge_recv.at[number],
-            device_id=(elem, o, r), device_id_type=MESH,
-        )
-
-    edges = [
-        edge_copy(0, canon.at[o, 1:9, 64:80], got.at[1:9, 64:80]),
-        edge_copy(1, tops.at[1:9], tops_in.at[1:9]),
-        edge_copy(2, canon.at[o, 0, 0:80], got.at[0, 0:80]),
-        edge_copy(3, tops.at[0], tops_in.at[0]),
-        edge_copy(4, ends, ends_in),
-    ]
-
     def fill_tops(a, carry):
         z_top = pack_top([canon[o, a, 80:88, tile(t)] for t in range(TILES)], zi, 1)
         y_top = pack_top([canon[o, a, 88:96, tile(t)] for t in range(TILES)], yi, 8)
@@ -540,38 +602,26 @@
         tops[a, 8:16] = packed
         return carry
 
-    edges[0].start()
+    steps(8, 5, 5, x_pack)
+    x_send(1)
+    y_rows.start()
     steps(1, NODES - 2, NODES - 2, fill_tops)
-    lax.fori_loop(near + 4, near + 5, inner_done, 0)
-    edges[1].start()
-
-    for way in range(2):
-        @pl.when(x_links[1 - way][1])
-        def _(copy=x_copies[way]):
-            copy.wait_recv()
-
-
-    def x_unpack(block, carry):
-        here = pl.ds(block * 8, 8)
-        below = xr[0, here]
-        above = xr[1, here]
-        low = (jnp.where(low_half, below, zero), jnp.where(low_half, roll_lanes(below, 64), zero))
-        top = (jnp.where(low_half, zero, roll_lanes(above, 64)), jnp.where(low_half, zero, above))
-        for q in range(2):
-            canon[q, 0, here, tile(0)] = canon[q, 0, here, tile(0)] + low[q]
-            canon[q, 9, here, tile(2)] = canon[q, 9, here, tile(2)] + top[q]
-        return carry
-
-    steps(0, ROWS // 8, 13, x_unpack)
-    edges[2].start()
+    steps(8, 5, 5, x_pass)
+    most_tops.start()
+    x_wait(0)
+    steps(0, 8, 8, x_unpack)
+    x_inner.start()
+    lax.fori_loop(near + 2, near + 5, inner_done, 0)
+    x_wait(1)
+    steps(8, 5, 5, x_unpack)
+    x_edges.start()
     fill_tops(0, 0)
     blocks = [canon[o, 9, k * 8 : k * 8 + 8, tile(2)] for k in range(ROWS // 8)] + [zero]
     for k in range(7):
         ends[k * 8 : k * 8 + 8] = jnp.where(low_half, roll_lanes(blocks[k], 64), blocks[k + 7])
-    lax.fori_loop(far, far + 1, inner_done, 0)
-    edges[3].start()
-    edges[4].start()
-    lax.fori_loop(far + 1, far + 5, inner_done, 0)
+    x_tops.start()
+    x_ends.start()
+    lax.fori_loop(far, far + HALF, inner_done, 0)
 
     def complete(a, carry):
         for t in range(TILES):
@@ -589,8 +639,7 @@
             got[a, 96:104, tile(t)] = jnp.where(row < 2, full, jnp.where(row < 4, after, zero))
         return carry
 
-    for number in range(2):
-        edges[number].wait_recv()
+    whole_groups[0].wait_recv()
     steps(1, NODES - 2, NODES - 2, complete)
 
     def pair_done(pair, carry):
@@ -603,8 +652,7 @@
 
     lax.fori_loop(0, 2, pair_done, 0)
 
-    for number in range(2, 5):
-        edges[number].wait_recv()
+    whole_groups[1].wait_recv()
     complete(0, 0)
 
     for k in range(ROWS // 8):
@@ -624,19 +672,22 @@
         put_edges(a, value, 64)
 
     z_copy.wait_send()
-    for copy in edges:
-        copy.wait_send()
-    for links, copies in ((y_links, y_copies), (x_links, x_copies)):
-        for way in range(2):
-            @pl.when(links[way][1])
-            def _(copy=copies[way]):
-                copy.wait_send()
-
-    def sent(a, carry):
-        inner_copy(a).wait_send()
-        return carry
-
-    lax.fori_loop(1, NODES - 1, sent, 0)
+    for way in range(2):
+        @pl.when(y_links[way][1])
+        def _(copy=y_copies[way]):
+            copy.wait_send()
+
+        @pl.when(x_links[way][1])
+        def _(way=way):
+            for part in range(2):
+                x_copy(part, way).wait_send()
+
+    for group in whole_groups:
+        group.wait_send()
+    pltpu.make_async_remote_copy(
+        src_ref=raw.at[o, 1:9, 0:64], dst_ref=got.at[1:9, 0:64], send_sem=send_sem.at[0], recv_sem=inner_sem.at[0],
+        device_id=(elem, o, r), device_id_type=MESH,
+    ).wait_send()
 
 
 def body(velocity, geometry, element_place):
@@ -657,6 +708,7 @@
             vmem((3, 3, HALF, NODES, NODES, 2, ELEMS), f32),
             pltpu.SMEM((2 * HALF * HALF,), f32),
             vmem((HALF, NODES, NODES, 2, ELEMS), f32),
+            vmem((HALF, NODES, NODES, 2, ELEMS), f32),
             vmem((NODES, NODES, 2, ELEMS), f32),
             vmem((2, 2 * ELEMS, ELEMS), jnp.bfloat16),
             vmem((2 * ELEMS, ELEMS), jnp.bfloat16),
@@ -666,16 +718,16 @@
             vmem((NODES, ROWS, ELEMS), f32),
             vmem((2, NODES, 16, LANES), f32),
             vmem((2, NODES, 16, LANES), f32),
-            vmem((2, NODES, 16, LANES), f32),
-            vmem((2, NODES, 16, LANES), f32),
+            vmem((2, ROWS, LANES), f32),
+            vmem((2, ROWS, LANES), f32),
             vmem((2, ROWS, LANES), f32),
             vmem((2, ROWS, LANES), f32),
             vmem((NODES - 1, 16, LANES), f32),
             vmem((NODES - 1, 16, LANES), f32),
             vmem((56, LANES), f32),
             vmem((56, LANES), f32),
-            dma((HALF,)), dma((3, HALF)), dma((2,)), dma((2,)), dma((2, 2)), dma((2, 2)),
-            dma((NODES,)), dma((NODES,)), dma((5,)), dma((5,)),
+            dma((2, HALF)), dma((HALF,)), dma((2,)), dma((2,)), dma((2, 2)), dma((2, 2, 2)),
+            dma((3,)), dma((8,)), dma((2,)),
         ],
         compiler_params=pltpu.CompilerParams(
             collective_id=0, has_side_effects=True, vmem_limit_bytes=60 * 1024 * 1024

time: 39.8 us -> 36.3 us (0.912)
  the two profiles are of different devices: /device:TPU:39 before, /device:TPU:100 now
where the time goes in v3:
time: 36.3 us; the launch traced here: 36.2 us
  Pallas kernels  35.1 us (97%)
  local copies, waits for them, and re-layouts  1.13 us (3%)
    pallas_call x1, Pallas kernels, body(): pl.pallas_call(kernel, out_shape=pltpu.VMEM((NODES * NODES * NODES * TILE...  35.1 us
    unnamed x1, local copies, waits for them, and re-layouts  1.13 us

profile of v3, /device:TPU:100, one launch (start us, length us, event | category | flops | bytes accessed | tf_op | source)
XLA Modules:
  0.0 36.2 jit_solution(8483090297331541899)
XLA Ops:
  0.0 35.1 %shard_map.37 = f32[3000,128]{1,0:T(8,128)S(1)} custom-call(f32[3,5,10,10,2,384]{5,4,3,2,1,0:T(2,128)} %v_hbm.1, f32[3,3,5,10,10,2,384]{6,5,4,3,2,1,0:T(2,128)} %g_hbm.1, s32[1,384]{1,0:T(1,128)} %place_ref.1), custom_call_target="tpu_custom_call" | custom-call | tf_op jit(solution)/shard_map/pallas_call | solution.py:697
  35.1 1.1 %copy.7 = f32[10,10,10,1,384]{4,3,2,1,0:T(1,128)} copy(f32[10,10,10,1,384]{4,3,2,1,0:T(1,128)S(1)} %bitcast.1) | data formatting | bytes 3072000

commit v4 on v3

--- a/solution.py
+++ b/solution.py
@@ -10,6 +10,7 @@
 BLOCK_Y = 8
 BLOCK_Z = 8
 GRID_Y = 4
+RING_Y = 4
 NODES = 10
 HALF = 5
 ELEMS = 384
@@ -118,8 +119,10 @@
     grid_x = elem_count // GRID_Y
     sx = elem // GRID_Y
     sy = elem % GRID_Y
-    y_links = ((elem + 1, sy < GRID_Y - 1), (elem - 1, sy > 0))
-    x_links = ((elem + GRID_Y, sx < grid_x - 1), (elem - GRID_Y, sx > 0))
+    y_links = (((elem + 1, c, r), sy < GRID_Y - 1), ((elem - 1, c, r), sy > 0))
+    up_comp = jnp.where(sx % RING_Y == RING_Y - 1, o, c)
+    down_comp = jnp.where(sx % RING_Y == 0, o, c)
+    x_links = (((elem + GRID_Y, up_comp, r), sx < grid_x - 1), ((elem - GRID_Y, down_comp, r), sx > 0))
 
     def first_copies(i, half):
         here = slice(half * HALF, half * HALF + HALF)
@@ -143,19 +146,12 @@
     expected = 2
     for other in ((elem, o, r), (elem, c, 1 - r)):
         pl.semaphore_signal(barrier, inc=1, device_id=other, device_id_type=MESH)
-    for near_elem, exists in y_links + x_links:
+    for neighbour, exists in y_links + x_links:
         expected = expected + exists.astype(jnp.int32)
 
         @pl.when(exists)
-        def _(near_elem=near_elem):
-            pl.semaphore_signal(barrier, inc=1, device_id=(near_elem, c, r), device_id_type=MESH)
-
-    pl.semaphore_wait(barrier, expected)
-    place_copy = pltpu.make_async_remote_copy(
-        src_ref=place_ref, dst_ref=place_in, send_sem=place_sem.at[0], recv_sem=place_sem.at[1],
-        device_id=(elem, o, r), device_id_type=MESH,
-    )
-    place_copy.start()
+        def _(neighbour=neighbour):
+            pl.semaphore_signal(barrier, inc=1, device_id=neighbour, device_id_type=MESH)
 
     for links, target in ((y_links, yr), (x_links, xr)):
         for way in range(2):
@@ -273,13 +269,17 @@
         return carry
 
     lax.fori_loop(0, HALF, first_flux(0), 0)
+    pl.semaphore_wait(barrier, expected)
+    place_copy = pltpu.make_async_remote_copy(
+        src_ref=place_ref, dst_ref=place_in, send_sem=place_sem.at[0], recv_sem=place_sem.at[1],
+        device_id=(elem, o, r), device_id_type=MESH,
+    )
+    place_copy.start()
     lax.fori_loop(0, HALF, far_first, 0)
     lax.fori_loop(0, HALF, first_flux(1), 0)
     lax.fori_loop(0, HALF, far_second, 0)
-    place_copy.wait()
-    fill_perm(o, place_in[...])
-
-    def near_plane(m, carry):
+
+    def near_plane(m):
         later_copy(m).wait()
 
         def flux(j, b, k):
@@ -307,25 +307,28 @@
 
         steps(0, NODES, 2, at_k)
 
-        def between():
-            gather_inner(m, near + m, 0)
-            gather_inner(m, near + m, 1)
-            gather_edges(m, near + m)
-
-        to_canon(far + m, between)
-
-        @pl.when(m < 3 - c)
-        def _():
-            send_inner(near + m, (0, 1))
-
-        return carry
-
-    lax.fori_loop(0, HALF, near_plane, 0)
-
+    def near_gather(m):
+        gather_inner(m, near + m, 0)
+        gather_inner(m, near + m, 1)
+        gather_edges(m, near + m)
+
+    def near_step(m, carry):
+        near_plane(m)
+        to_canon(far + m - c, lambda: near_gather(m))
+        send_inner(near + m, (0, 1))
+        return carry
+
+    near_plane(0)
+    near_gather(0)
+    send_inner(near, (0, 1))
+    place_copy.wait()
+    fill_perm(o, place_in[...])
+    lax.fori_loop(1, HALF, near_step, 0)
+    six_planes = pl.ds(near - c, HALF + 1)
     for q in range(2):
-        canon[q, pl.ds(near, HALF), 64:104] = permuted(
-            raw[q, pl.ds(near, HALF), 64:104].reshape(HALF * 40, ELEMS), perm[q]
-        ).reshape(HALF, 40, ELEMS)
+        canon[q, six_planes, 64:104] = permuted(
+            raw[q, six_planes, 64:104].reshape((HALF + 1) * 40, ELEMS), perm[q]
+        ).reshape(HALF + 1, 40, ELEMS)
 
     lane = lax.broadcasted_iota(jnp.int32, (8, LANES), 1)
     row = lax.broadcasted_iota(jnp.int32, (8, LANES), 0)
@@ -339,8 +342,8 @@
     b_hi = jnp.logical_or(row == 2, row == 3)
 
     def line_pass(lo_row, index, shift, corner_lo, corner_hi, corner_step):
-        def two_planes(step, carry):
-            spots = [(q, 2 * step + k, tile(t)) for k in range(2) for q in range(2) for t in range(TILES)]
+        def two_planes(planes):
+            spots = [(q, a, tile(t)) for a in planes for q in range(2) for t in range(TILES)]
             corners = [canon[q, a, 96:104, lanes] for q, a, lanes in spots]
             lows = [canon[q, a, lo_row : lo_row + 8, lanes] for q, a, lanes in spots]
             highs = [canon[q, a, lo_row + 16 : lo_row + 24, lanes] for q, a, lanes in spots]
@@ -358,9 +361,15 @@
                         jnp.logical_and(corner_hi, index < 7), roll_lanes(roll_rows(k, corner_step), -shift), zero
                     )
                 )
+
+        return two_planes
+
+    def over_middle(pass_over):
+        def at_step(step, carry):
+            pass_over([1 + 2 * step, 2 + 2 * step])
             return carry
 
-        return two_planes
+        lax.fori_loop(0, 4, at_step, 0)
 
     z_pass = line_pass(64, zi, 1, c_lo, c_hi, 1)
     y_pass = line_pass(72, yi, 8, b_lo, b_hi, 2)
@@ -395,20 +404,25 @@
     def on(flag):
         return jnp.where(flag, 1.0, 0.0).astype(jnp.float32)
 
-    def z_pack(a, carry):
-        corner = six(a, slice(96, 104))
-        zs[0, a, 0:8] = pack_top(six(a, slice(80, 88)), zi, 1)
-        zs[0, a, 8:16] = pack_top(corner, zi, 1)
-        zs[1, a, 0:8] = pack_low(six(a, slice(64, 72)), zi, 1)
-        zs[1, a, 8:16] = pack_low(corner, zi, 1)
-        return carry
-
-    steps(0, NODES, NODES, z_pack)
-    z_copy = pltpu.make_async_remote_copy(
-        src_ref=zs, dst_ref=zr, send_sem=z_sem.at[0], recv_sem=z_sem.at[1],
-        device_id=(elem, c, 1 - r), device_id_type=MESH,
-    )
-    z_copy.start()
+    middle, ends_planes = tuple(range(1, 9)), (0, 9)
+    slots = {a: (a - 1 if 0 < a < 9 else 8 + a // 9) for a in range(NODES)}
+
+    def z_pack(planes):
+        for a in planes:
+            corner = six(a, slice(96, 104))
+            zs[0, slots[a], 0:8] = pack_top(six(a, slice(80, 88)), zi, 1)
+            zs[0, slots[a], 8:16] = pack_top(corner, zi, 1)
+            zs[1, slots[a], 0:8] = pack_low(six(a, slice(64, 72)), zi, 1)
+            zs[1, slots[a], 8:16] = pack_low(corner, zi, 1)
+
+    def z_copy(part):
+        here = slice(0, 8) if part == 0 else slice(8, 10)
+        return pltpu.make_async_remote_copy(
+            src_ref=zs.at[:, here], dst_ref=zr.at[:, here], send_sem=z_sem.at[0, part], recv_sem=z_sem.at[1, part],
+            device_id=(elem, c, 1 - r), device_id_type=MESH,
+        )
+
+    r0, r1 = on(r == 0), on(r == 1)
 
     def x_pack(block, carry):
         here = pl.ds(block * 8, 8)
@@ -416,24 +430,30 @@
         xs[1, here] = jnp.where(low_half, canon[0, 0, here, tile(0)], roll_lanes(canon[1, 0, here, tile(0)], 64))
         return carry
 
-    def x_copy(part, way):
-        rows = slice(0, 64) if part == 0 else slice(64, ROWS)
+    def x_copy(way):
         return pltpu.make_async_remote_copy(
-            src_ref=xs.at[way, rows], dst_ref=xr.at[way, rows],
-            send_sem=x_sem.at[0, part, way], recv_sem=x_sem.at[1, part, way],
-            device_id=(x_links[way][0], c, r), device_id_type=MESH,
+            src_ref=xs.at[way], dst_ref=xr.at[way], send_sem=x_sem.at[0, way], recv_sem=x_sem.at[1, way],
+            device_id=x_links[way][0], device_id_type=MESH,
         )
 
-    def x_send(part):
+    def y_copy(part, way):
+        here = slice(0, 80) if part == 0 else slice(80, 104)
+        return pltpu.make_async_remote_copy(
+            src_ref=ys.at[way, here], dst_ref=yr.at[way, here],
+            send_sem=y_sem.at[0, part, way], recv_sem=y_sem.at[1, part, way],
+            device_id=y_links[way][0], device_id_type=MESH,
+        )
+
+    def send_both(links, copies):
         for way in range(2):
-            @pl.when(x_links[way][1])
-            def _(copy=x_copy(part, way)):
+            @pl.when(links[way][1])
+            def _(copy=copies[way]):
                 copy.start()
 
-    def x_wait(part):
+    def wait_both(links, copies):
         for way in range(2):
-            @pl.when(x_links[1 - way][1])
-            def _(copy=x_copy(part, way)):
+            @pl.when(links[1 - way][1])
+            def _(copy=copies[way]):
                 copy.wait_recv()
 
     def x_unpack(block, carry):
@@ -482,15 +502,14 @@
         both = permuted(both, perm[q])
         canon[q, 0, 0:64] = both[0:64]
         canon[q, 9, 0:64] = both[64:128]
-    steps(0, 8, 8, x_pack)
-    x_send(0)
-
-    def send_late(a, carry):
-        send_inner(a, (0, 1))
-        return carry
-
-    lax.fori_loop(near + 3 - c, near + HALF, send_late, 0)
-    lax.fori_loop(0, NODES // 2, z_pass, 0)
+    steps(0, ROWS // 8, 13, x_pack)
+    send_both(x_links, [x_copy(way) for way in range(2)])
+
+    z_pack(middle)
+    z_copy(0).start()
+    over_middle(z_pass)
+    steps(0, ROWS // 8, 13, x_pass)
+
     def edge_copy(group, source, target):
         return pltpu.make_async_remote_copy(
             src_ref=source, dst_ref=target, send_sem=send_sem.at[group + 1], recv_sem=edge_sem.at[group],
@@ -509,12 +528,10 @@
         edge_copy(1, canon.at[o, 9], got.at[9]),
     )
 
-    z_copy.wait_recv()
-    r0, r1 = on(r == 0), on(r == 1)
-
     def z_unpack(a, carry):
-        tops_here = [zr[0, a, 0:8], roll_rows(zr[0, a, 8:16], -1)]
-        lows_here = [zr[1, a, 0:8], roll_rows(zr[1, a, 8:16], 1)]
+        slot = slots[a]
+        tops_here = [zr[0, slot, 0:8], roll_rows(zr[0, slot, 8:16], -1)]
+        lows_here = [zr[1, slot, 0:8], roll_rows(zr[1, slot, 8:16], 1)]
         for t in range(TILES):
             for kind in range(2):
                 top_rows = slice(80, 88) if kind == 0 else slice(96, 104)
@@ -533,48 +550,28 @@
                     canon[q, a, rows, tile(t)] = canon[q, a, rows, tile(t)] + jnp.where(mask, value, zero)
         return carry
 
-    steps(0, NODES, NODES, z_unpack)
-
-    z_rows.start()
-
-    for a in range(NODES):
-        ys[0, a * 8 : a * 8 + 8] = pack_top(six(a, slice(88, 96)), yi, 8)
-        ys[1, a * 8 : a * 8 + 8] = pack_low(six(a, slice(72, 80)), yi, 8)
-    for group in range(3):
-        top_total, low_total = zero, zero
-        for k, a in enumerate(range(4 * group, min(4 * group + 4, NODES))):
-            corner = six(a, slice(96, 104))
-            mine = row // 2 == k
-            top_total = jnp.where(mine, roll_rows(pack_top(corner, yi, 8), 2 * k - 2), top_total)
-            low_total = jnp.where(mine, roll_rows(pack_low(corner, yi, 8), 2 * k), low_total)
-        ys[0, 80 + group * 8 : 88 + group * 8] = top_total
-        ys[1, 80 + group * 8 : 88 + group * 8] = low_total
-    y_copies = [
-        pltpu.make_async_remote_copy(
-            src_ref=ys.at[way], dst_ref=yr.at[way], send_sem=y_sem.at[0, way], recv_sem=y_sem.at[1, way],
-            device_id=(y_links[way][0], c, r), device_id_type=MESH,
-        )
-        for way in range(2)
-    ]
-    for way in range(2):
-        @pl.when(y_links[way][1])
-        def _(copy=y_copies[way]):
-            copy.start()
-
-
-    lax.fori_loop(0, NODES // 2, y_pass, 0)
-    steps(0, 8, 8, x_pass)
-    lax.fori_loop(near, near + 2, inner_done, 0)
-    for way in range(2):
-        @pl.when(y_links[1 - way][1])
-        def _(copy=y_copies[way]):
-            copy.wait_recv()
-
+    def y_pack(planes, first):
+        for k, a in enumerate(planes):
+            here = slice(first + k * 8, first + k * 8 + 8)
+            ys[0, here] = pack_top(six(a, slice(88, 96)), yi, 8)
+            ys[1, here] = pack_low(six(a, slice(72, 80)), yi, 8)
+        for group in range(0, len(planes), 4):
+            top_total, low_total = zero, zero
+            for k, a in enumerate(planes[group : group + 4]):
+                corner = six(a, slice(96, 104))
+                mine = row // 2 == k
+                top_total = jnp.where(mine, roll_rows(pack_top(corner, yi, 8), 2 * k - 2), top_total)
+                low_total = jnp.where(mine, roll_rows(pack_low(corner, yi, 8), 2 * k), low_total)
+            here = slice(first + len(planes) * 8 + group * 2, first + len(planes) * 8 + group * 2 + 8)
+            ys[0, here] = top_total
+            ys[1, here] = low_total
 
     def y_unpack(a, carry):
-        group, k = 80 + a // 4 * 8, a % 4
-        below = [yr[0, a * 8 : a * 8 + 8], roll_rows(yr[0, group : group + 8], -2 * k)]
-        above = [yr[1, a * 8 : a * 8 + 8], roll_rows(yr[1, group : group + 8], 2 - 2 * k)]
+        place, first, count = (a - 1, 0, 8) if 0 < a < 9 else (a // 9, 80, 2)
+        here = slice(first + place * 8, first + place * 8 + 8)
+        group, k = first + count * 8 + place // 4 * 8, place % 4
+        below = [yr[0, here], roll_rows(yr[0, group : group + 8], -2 * k)]
+        above = [yr[1, here], roll_rows(yr[1, group : group + 8], 2 - 2 * k)]
         for q in range(2):
             for t in range(TILES):
                 u = 3 * q + t
@@ -589,7 +586,6 @@
                     canon[q, a, low_rows, tile(t)] = canon[q, a, low_rows, tile(t)] + down
         return carry
 
-    steps(0, NODES, NODES, y_unpack)
 
     def fill_tops(a, carry):
         z_top = pack_top([canon[o, a, 80:88, tile(t)] for t in range(TILES)], zi, 1)
@@ -602,18 +598,38 @@
         tops[a, 8:16] = packed
         return carry
 
-    steps(8, 5, 5, x_pack)
-    x_send(1)
+    z_copy(0).wait_recv()
+    for a in middle:
+        z_unpack(a, 0)
+    z_rows.start()
+    y_pack(middle, 0)
+    send_both(y_links, [y_copy(0, way) for way in range(2)])
+    over_middle(y_pass)
+    lax.fori_loop(near, near + 2, inner_done, 0)
+    wait_both(y_links, [y_copy(0, way) for way in range(2)])
+    for a in middle:
+        y_unpack(a, 0)
     y_rows.start()
     steps(1, NODES - 2, NODES - 2, fill_tops)
-    steps(8, 5, 5, x_pass)
     most_tops.start()
-    x_wait(0)
-    steps(0, 8, 8, x_unpack)
+
+    wait_both(x_links, [x_copy(way) for way in range(2)])
+    steps(0, ROWS // 8, 13, x_unpack)
     x_inner.start()
-    lax.fori_loop(near + 2, near + 5, inner_done, 0)
-    x_wait(1)
-    steps(8, 5, 5, x_unpack)
+    z_pack(ends_planes)
+    z_copy(1).start()
+    z_pass(ends_planes)
+    lax.fori_loop(near + 2, near + 4, inner_done, 0)
+    z_copy(1).wait_recv()
+    for a in ends_planes:
+        z_unpack(a, 0)
+    y_pack(ends_planes, 80)
+    send_both(y_links, [y_copy(1, way) for way in range(2)])
+    y_pass(ends_planes)
+    lax.fori_loop(near + 4, near + HALF, inner_done, 0)
+    wait_both(y_links, [y_copy(1, way) for way in range(2)])
+    for a in ends_planes:
+        y_unpack(a, 0)
     x_edges.start()
     fill_tops(0, 0)
     blocks = [canon[o, 9, k * 8 : k * 8 + 8, tile(2)] for k in range(ROWS // 8)] + [zero]
@@ -671,16 +687,17 @@
                 put(a, b + 1, value, t, b * 8)
         put_edges(a, value, 64)
 
-    z_copy.wait_send()
+    for part in range(2):
+        z_copy(part).wait_send()
     for way in range(2):
         @pl.when(y_links[way][1])
-        def _(copy=y_copies[way]):
-            copy.wait_send()
+        def _(way=way):
+            for part in range(2):
+                y_copy(part, way).wait_send()
 
         @pl.when(x_links[way][1])
         def _(way=way):
-            for part in range(2):
-                x_copy(part, way).wait_send()
+            x_copy(way).wait_send()
 
     for group in whole_groups:
         group.wait_send()
@@ -726,7 +743,7 @@
             vmem((NODES - 1, 16, LANES), f32),
             vmem((56, LANES), f32),
             vmem((56, LANES), f32),
-            dma((2, HALF)), dma((HALF,)), dma((2,)), dma((2,)), dma((2, 2)), dma((2, 2, 2)),
+            dma((2, HALF)), dma((HALF,)), dma((2,)), dma((2, 2)), dma((2, 2, 2)), dma((2, 2)),
             dma((3,)), dma((8,)), dma((2,)),
         ],
         compiler_params=pltpu.CompilerParams(

time: 36.3 us -> 33.8 us (0.931)
  the two profiles are of different devices: /device:TPU:100 before, /device:TPU:1 now
where the time goes in v4:
time: 33.8 us; the launch traced here: 33.7 us
  Pallas kernels  32.6 us (96%)
  local copies, waits for them, and re-layouts  1.13 us (3%)
    pallas_call x1, Pallas kernels, body(): pl.pallas_call(kernel, out_shape=pltpu.VMEM((NODES * NODES * NODES * TILE...  32.6 us
    unnamed x1, local copies, waits for them, and re-layouts  1.13 us

profile of v4, /device:TPU:1, one launch (start us, length us, event | category | flops | bytes accessed | tf_op | source)
XLA Modules:
  0.0 33.7 jit_solution(9780574417922734718)
XLA Ops:
  0.0 32.6 %shard_map.37 = f32[3000,128]{1,0:T(8,128)S(1)} custom-call(f32[3,5,10,10,2,384]{5,4,3,2,1,0:T(2,128)} %v_hbm.1, f32[3,3,5,10,10,2,384]{6,5,4,3,2,1,0:T(2,128)} %g_hbm.1, s32[1,384]{1,0:T(1,128)} %place_ref.1), custom_call_target="tpu_custom_call" | custom-call | tf_op jit(solution)/shard_map/pallas_call | solution.py:714
  32.6 1.1 %copy.7 = f32[10,10,10,1,384]{4,3,2,1,0:T(1,128)} copy(f32[10,10,10,1,384]{4,3,2,1,0:T(1,128)S(1)} %bitcast.1) | data formatting | bytes 3072000

commit v5 on v4

--- a/solution.py
+++ b/solution.py
@@ -11,6 +11,8 @@
 BLOCK_Z = 8
 GRID_Y = 4
 RING_Y = 4
+PART_ROWS = ((1, 2, 3), (4, 5, 6, 7, 8, 9, 0))
+PART_INNER = (slice(0, 24), slice(24, 64))
 NODES = 10
 HALF = 5
 ELEMS = 384
@@ -106,8 +108,8 @@
 
 
 def kernel(
-    v_hbm, g_hbm, place_ref, out_ref,
-    v, g, coef, f0, fl, fn, perm, back, place_in, raw, canon, got,
+    v_hbm, g_hbm, place_hbm, out_ref,
+    v, g, coef, f0, fl, fn, perm, back, place_own, place_in, raw, canon, got,
     zs, zr, ys, yr, xs, xr, tops, tops_in, ends, ends_in,
     first_sem, later_sem, place_sem, z_sem, y_sem, x_sem, send_sem, inner_sem, edge_sem,
 ):
@@ -124,24 +126,6 @@
     down_comp = jnp.where(sx % RING_Y == 0, o, c)
     x_links = (((elem + GRID_Y, up_comp, r), sx < grid_x - 1), ((elem - GRID_Y, down_comp, r), sx > 0))
 
-    def first_copies(i, half):
-        here = slice(half * HALF, half * HALF + HALF)
-        return (
-            pltpu.make_async_copy(v_hbm.at[:, i, here], v.at[:, i, here], first_sem.at[half, i]),
-            pltpu.make_async_copy(g_hbm.at[:, 0, i, here], g.at[:, 0, i, here], first_sem.at[half, i]),
-        )
-
-    def first_arrived(i, half):
-        here = slice(half * HALF, half * HALF + HALF)
-        pltpu.make_async_copy(g_hbm.at[:, 0:2, i, here], g.at[:, 0:2, i, here], first_sem.at[half, i]).wait()
-
-    def later_copy(i):
-        return pltpu.make_async_copy(g_hbm.at[:, 1:3, i], g.at[:, 1:3, i], later_sem.at[i])
-
-    for i in range(HALF):
-        for copy in first_copies(i, 0):
-            copy.start()
-
     barrier = pltpu.get_barrier_semaphore()
     expected = 2
     for other in ((elem, o, r), (elem, c, 1 - r)):
@@ -153,6 +137,29 @@
         def _(neighbour=neighbour):
             pl.semaphore_signal(barrier, inc=1, device_id=neighbour, device_id_type=MESH)
 
+    own_copy = pltpu.make_async_copy(place_hbm, place_own, place_sem.at[2])
+    own_copy.start()
+
+    def first_copies(i, part):
+        copies = []
+        for here in (slice(1, 4),) if part == 0 else (slice(4, 10), slice(0, 1)):
+            copies.append(pltpu.make_async_copy(v_hbm.at[:, i, here], v.at[:, i, here], first_sem.at[part, i]))
+            copies.append(
+                pltpu.make_async_copy(g_hbm.at[:, 0, i, here], g.at[:, 0, i, here], first_sem.at[part, i])
+            )
+        return copies
+
+    def first_arrived(i, part):
+        here = slice(0, len(PART_ROWS[part]))
+        pltpu.make_async_copy(g_hbm.at[:, 0:2, i, here], g.at[:, 0:2, i, here], first_sem.at[part, i]).wait()
+
+    def later_copy(i):
+        return pltpu.make_async_copy(g_hbm.at[:, 1:3, i], g.at[:, 1:3, i], later_sem.at[i])
+
+    for i in range(HALF):
+        for copy in first_copies(i, 0):
+            copy.start()
+
     for links, target in ((y_links, yr), (x_links, xr)):
         for way in range(2):
             @pl.when(jnp.logical_not(links[1 - way][1]))
@@ -166,6 +173,8 @@
                 second = float(TABLE[5 + i, m if kind == 0 else (5 + m)])
                 coef[(kind * HALF + m) * HALF + i] = jnp.where(c == 0, first, second).astype(jnp.float32)
 
+
+    own_copy.wait()
     rows_iota = lax.broadcasted_iota(jnp.int32, (ELEMS, ELEMS), 0)
     lanes_iota = lax.broadcasted_iota(jnp.int32, (LANES, ELEMS), 1).astype(jnp.float32)
 
@@ -177,29 +186,29 @@
             for copy in range(2):
                 perm[q, copy * ELEMS + t * LANES : copy * ELEMS + (t + 1) * LANES, :] = part
 
-    back_half = jnp.where(rows_iota == place_ref[...], 1.0, 0.0).astype(jnp.bfloat16)
+    back_half = jnp.where(rows_iota == place_own[...], 1.0, 0.0).astype(jnp.bfloat16)
     back[0:ELEMS, :] = back_half
     back[ELEMS : 2 * ELEMS, :] = back_half
-    fill_perm(c, place_ref[...])
+    fill_perm(c, place_own[...])
     raw[:, :, 96:104] = jnp.zeros((2, NODES, 8, ELEMS), jnp.float32)
 
     far = HALF * o
     near = HALF * c
 
-    def inner_copy(a, rows):
+    def inner_copy(a, rows, group):
         return pltpu.make_async_remote_copy(
-            src_ref=raw.at[o, a, rows], dst_ref=got.at[a, rows], send_sem=send_sem.at[0], recv_sem=inner_sem.at[a - 1],
+            src_ref=raw.at[o, a, rows], dst_ref=got.at[a, rows], send_sem=send_sem.at[0], recv_sem=inner_sem.at[group],
             device_id=(elem, o, r), device_id_type=MESH,
         )
 
     def is_inner(a):
         return jnp.logical_and(a > 0, a < NODES - 1)
 
-    def send_inner(a, halves):
+    def send_inner(a, halves, group):
         @pl.when(is_inner(a))
         def _():
             for half in halves:
-                inner_copy(a, slice(half * 32, half * 32 + 32)).start()
+                inner_copy(a, PART_INNER[half], group).start()
 
     def first_flux(half):
         def at_plane(i, carry):
@@ -215,7 +224,7 @@
                         + g[2, 0, i, b, k] * v[2, i, b, k]
                     )
 
-            for b in range(half * HALF, half * HALF + HALF):
+            for b in PART_ROWS[half]:
                 at_b(b, 0)
             return carry
 
@@ -223,14 +232,14 @@
 
     def mix_planes(m, half):
         weights = [coef[m * HALF + i] for i in range(HALF)]
-        for b in range(half * HALF, half * HALF + HALF):
+        for b in PART_ROWS[half]:
             for k in range(NODES):
                 fl[m, b, k] = weighted([f0[i, b, k] for i in range(HALF)], weights)
 
     def gather_inner(m, a, half):
         for q in range(2):
             for t in range(TILES):
-                for b in range(half * 4, half * 4 + 4):
+                for b in range(PART_INNER[half].start // 8, PART_INNER[half].stop // 8):
                     raw[q, a, b * 8 : b * 8 + 8, tile(t)] = fl[m, b + 1, 1:9, q, tile(t)]
 
     def gather_edges(m, a):
@@ -255,23 +264,25 @@
         for q in range(2):
             canon[q, a, 64:104] = jnp.dot(parts[q], perm[q], preferred_element_type=jnp.float32)
 
-    def far_first(m, carry):
+    def far_first(step, carry):
+        m = (step + c) % HALF
         mix_planes(m, 0)
         gather_inner(m, far + m, 0)
-        send_inner(far + m, (0,))
-        return carry
-
-    def far_second(m, carry):
+        send_inner(far + m, (0,), 0)
+        return carry
+
+    def far_second(step, carry):
+        m = (step + c) % HALF
         mix_planes(m, 1)
         gather_inner(m, far + m, 1)
-        send_inner(far + m, (1,))
+        send_inner(far + m, (1,), 0)
         gather_edges(m, far + m)
         return carry
 
     lax.fori_loop(0, HALF, first_flux(0), 0)
     pl.semaphore_wait(barrier, expected)
     place_copy = pltpu.make_async_remote_copy(
-        src_ref=place_ref, dst_ref=place_in, send_sem=place_sem.at[0], recv_sem=place_sem.at[1],
+        src_ref=place_own, dst_ref=place_in, send_sem=place_sem.at[0], recv_sem=place_sem.at[1],
         device_id=(elem, o, r), device_id_type=MESH,
     )
     place_copy.start()
@@ -315,12 +326,12 @@
     def near_step(m, carry):
         near_plane(m)
         to_canon(far + m - c, lambda: near_gather(m))
-        send_inner(near + m, (0, 1))
+        send_inner(near + m, (0, 1), 1)
         return carry
 
     near_plane(0)
     near_gather(0)
-    send_inner(near, (0, 1))
+    send_inner(near, (0, 1), 1)
     place_copy.wait()
     fill_perm(o, place_in[...])
     lax.fori_loop(1, HALF, near_step, 0)
@@ -416,9 +427,9 @@
             zs[1, slots[a], 8:16] = pack_low(corner, zi, 1)
 
     def z_copy(part):
-        here = slice(0, 8) if part == 0 else slice(8, 10)
+        here = (slice(0, 8), slice(8, 10), slice(0, 10))[part]
         return pltpu.make_async_remote_copy(
-            src_ref=zs.at[:, here], dst_ref=zr.at[:, here], send_sem=z_sem.at[0, part], recv_sem=z_sem.at[1, part],
+            src_ref=zs.at[:, here], dst_ref=zr.at[:, here], send_sem=z_sem.at[2], recv_sem=z_sem.at[part % 2],
             device_id=(elem, c, 1 - r), device_id_type=MESH,
         )
 
@@ -437,10 +448,10 @@
         )
 
     def y_copy(part, way):
-        here = slice(0, 80) if part == 0 else slice(80, 104)
+        here = (slice(0, 80), slice(80, ROWS), slice(0, ROWS))[part]
         return pltpu.make_async_remote_copy(
             src_ref=ys.at[way, here], dst_ref=yr.at[way, here],
-            send_sem=y_sem.at[0, part, way], recv_sem=y_sem.at[1, part, way],
+            send_sem=y_sem.at[2, way], recv_sem=y_sem.at[part % 2, way],
             device_id=y_links[way][0], device_id_type=MESH,
         )
 
@@ -485,10 +496,12 @@
                 start = ((a * 10 + b) * 10 + k) * 3 + t
                 out_ref[pl.ds(start, 1), :] = value[first + 32 + number : first + 33 + number, tile(t)]
 
+    def inner_wait(group):
+        inner_copy(slice(1, 5), slice(0, 64), group).wait_recv()
+
     def inner_done(a, carry):
         @pl.when(is_inner(a))
         def _():
-            inner_copy(a, slice(0, 64)).wait_recv()
             for t in range(TILES):
                 value = got[a, 0:64, tile(t)] + raw[c, a, 0:64, tile(t)]
                 for b in range(8):
@@ -519,13 +532,15 @@
     z_rows = edge_copy(0, canon.at[o, 1:9, 64:72], got.at[1:9, 64:72])
     y_rows = edge_copy(0, canon.at[o, 1:9, 72:80], got.at[1:9, 72:80])
     most_tops = edge_copy(0, tops.at[1:9], tops_in.at[1:9])
-    x_inner = edge_copy(1, canon.at[o, 0, 0:64], got.at[0, 0:64])
+    x_inner = edge_copy(2, canon.at[o, 0, 0:64], got.at[0, 0:64])
     x_edges = edge_copy(1, canon.at[o, 0, 64:80], got.at[0, 64:80])
     x_tops = edge_copy(1, tops.at[0], tops_in.at[0])
-    x_ends = edge_copy(1, ends, ends_in)
+    x_ends_inner = edge_copy(2, ends.at[0:32], ends_in.at[0:32])
+    x_ends = edge_copy(1, ends.at[32:56], ends_in.at[32:56])
     whole_groups = (
         edge_copy(0, canon.at[o, 1:9, 0:64, 0:LANES], got.at[1:9, 0:64, 0:LANES]),
-        edge_copy(1, canon.at[o, 9], got.at[9]),
+        edge_copy(1, canon.at[o, 0, 0:88, 0:LANES], got.at[0, 0:88, 0:LANES]),
+        edge_copy(2, canon.at[o, 1:5, 0:56, 0:LANES], got.at[1:5, 0:56, 0:LANES]),
     )
 
     def z_unpack(a, carry):
@@ -598,6 +613,13 @@
         tops[a, 8:16] = packed
         return carry
 
+    def fill_ends(block, pairs, first):
+        for k in range(pairs):
+            low = canon[o, 9, (block + k) * 8 : (block + k) * 8 + 8, tile(2)]
+            high_block = block + k + pairs
+            high = canon[o, 9, high_block * 8 : high_block * 8 + 8, tile(2)] if high_block < ROWS // 8 else zero
+            ends[first + k * 8 : first + k * 8 + 8] = jnp.where(low_half, roll_lanes(low, 64), high)
+
     z_copy(0).wait_recv()
     for a in middle:
         z_unpack(a, 0)
@@ -605,6 +627,7 @@
     y_pack(middle, 0)
     send_both(y_links, [y_copy(0, way) for way in range(2)])
     over_middle(y_pass)
+    inner_wait(0)
     lax.fori_loop(near, near + 2, inner_done, 0)
     wait_both(y_links, [y_copy(0, way) for way in range(2)])
     for a in middle:
@@ -616,6 +639,8 @@
     wait_both(x_links, [x_copy(way) for way in range(2)])
     steps(0, ROWS // 8, 13, x_unpack)
     x_inner.start()
+    fill_ends(0, 4, 0)
+    x_ends_inner.start()
     z_pack(ends_planes)
     z_copy(1).start()
     z_pass(ends_planes)
@@ -632,11 +657,10 @@
         y_unpack(a, 0)
     x_edges.start()
     fill_tops(0, 0)
-    blocks = [canon[o, 9, k * 8 : k * 8 + 8, tile(2)] for k in range(ROWS // 8)] + [zero]
-    for k in range(7):
-        ends[k * 8 : k * 8 + 8] = jnp.where(low_half, roll_lanes(blocks[k], 64), blocks[k + 7])
+    fill_ends(8, 3, 32)
     x_tops.start()
     x_ends.start()
+    inner_wait(1)
     lax.fori_loop(far, far + HALF, inner_done, 0)
 
     def complete(a, carry):
@@ -668,32 +692,38 @@
 
     lax.fori_loop(0, 2, pair_done, 0)
 
+    def last_plane(block, pairs, first):
+        for k in range(block, min(block + 2 * pairs, ROWS // 8)):
+            here = slice(k * 8, k * 8 + 8)
+            start = first + (k - block) % pairs * 8
+            end = ends_in[start : start + 8]
+            lo = [roll_lanes(got[0, here, tile(t)], 64) for t in range(TILES)]
+            lo.append(roll_lanes(end, 64) if k < block + pairs else end)
+            for t in range(TILES):
+                got[9, here, tile(t)] = jnp.where(low_half, lo[t], lo[t + 1])
+
+    whole_groups[2].wait_recv()
+    last_plane(0, 4, 0)
+    total = jnp.concatenate([canon[c, a, 0:64] + got[a, 0:64] for a in (0, 9)], axis=0)
+    value = permuted(total, back[...])
+    for k, a in enumerate((0, 9)):
+        for t in range(TILES):
+            for b in range(8):
+                put(a, b + 1, value, t, k * 64 + b * 8)
+
     whole_groups[1].wait_recv()
     complete(0, 0)
-
-    for k in range(ROWS // 8):
-        here = slice(k * 8, k * 8 + 8)
-        end = ends_in[(k % 7) * 8 : (k % 7) * 8 + 8]
-        lo = [roll_lanes(got[0, here, tile(t)], 64) for t in range(TILES)]
-        lo.append(roll_lanes(end, 64) if k < 7 else end)
-        for t in range(TILES):
-            got[9, here, tile(t)] = jnp.where(low_half, lo[t], lo[t + 1])
-
-    for a in (0, 9):
-        total = canon[c, a] + got[a]
-        value = permuted(total, back[...])
-        for t in range(TILES):
-            for b in range(8):
-                put(a, b + 1, value, t, b * 8)
-        put_edges(a, value, 64)
-
-    for part in range(2):
-        z_copy(part).wait_send()
+    last_plane(8, 3, 32)
+    total = jnp.concatenate([canon[c, a, 64:104] + got[a, 64:104] for a in (0, 9)], axis=0)
+    value = permuted(total, back[...])
+    for k, a in enumerate((0, 9)):
+        put_edges(a, value, k * 40)
+
+    z_copy(2).wait_send()
     for way in range(2):
         @pl.when(y_links[way][1])
         def _(way=way):
-            for part in range(2):
-                y_copy(part, way).wait_send()
+            y_copy(2, way).wait_send()
 
         @pl.when(x_links[way][1])
         def _(way=way):
@@ -701,10 +731,7 @@
 
     for group in whole_groups:
         group.wait_send()
-    pltpu.make_async_remote_copy(
-        src_ref=raw.at[o, 1:9, 0:64], dst_ref=got.at[1:9, 0:64], send_sem=send_sem.at[0], recv_sem=inner_sem.at[0],
-        device_id=(elem, o, r), device_id_type=MESH,
-    ).wait_send()
+    inner_copy(slice(1, 9), slice(0, 64), 0).wait_send()
 
 
 def body(velocity, geometry, element_place):
@@ -717,7 +744,7 @@
         in_specs=[
             pl.BlockSpec(memory_space=pl.ANY),
             pl.BlockSpec(memory_space=pl.ANY),
-            pl.BlockSpec(memory_space=pltpu.VMEM),
+            pl.BlockSpec(memory_space=pl.ANY),
         ],
         out_specs=pl.BlockSpec(memory_space=pltpu.VMEM),
         scratch_shapes=[
@@ -729,6 +756,7 @@
             vmem((NODES, NODES, 2, ELEMS), f32),
             vmem((2, 2 * ELEMS, ELEMS), jnp.bfloat16),
             vmem((2 * ELEMS, ELEMS), jnp.bfloat16),
+            vmem((1, ELEMS), jnp.int32),
             vmem((1, ELEMS), jnp.int32),
             vmem((2, NODES, ROWS, ELEMS), f32),
             vmem((2, NODES, ROWS, ELEMS), f32),
@@ -743,8 +771,8 @@
             vmem((NODES - 1, 16, LANES), f32),
             vmem((56, LANES), f32),
             vmem((56, LANES), f32),
-            dma((2, HALF)), dma((HALF,)), dma((2,)), dma((2, 2)), dma((2, 2, 2)), dma((2, 2)),
-            dma((3,)), dma((8,)), dma((2,)),
+            dma((2, HALF)), dma((HALF,)), dma((3,)), dma((3,)), dma((3, 2)), dma((2, 2)),
+            dma((4,)), dma((2,)), dma((3,)),
         ],
         compiler_params=pltpu.CompilerParams(
             collective_id=0, has_side_effects=True, vmem_limit_bytes=60 * 1024 * 1024

time: 33.8 us -> 32.9 us (0.973)
  Pallas kernels: 32.6 us -> 31.6 us
    pallas_call x1, Pallas kernels: 32.6 us -> 31.6 us  [body(): pl.pallas_call(kernel, out_shape=pltpu.VMEM((NODES * NODES * NODES * TILE...]
where the time goes in v5:
time: 32.9 us; the launch traced here: 32.8 us
  Pallas kernels  31.6 us (96%)
  local copies, waits for them, and re-layouts  1.13 us (3%)
    pallas_call x1, Pallas kernels, body(): pl.pallas_call(kernel, out_shape=pltpu.VMEM((NODES * NODES * NODES * TILE...  31.6 us
    unnamed x1, local copies, waits for them, and re-layouts  1.13 us

profile of v5, /device:TPU:1, one launch (start us, length us, event | category | flops | bytes accessed | tf_op | source)
XLA Modules:
  0.0 32.8 jit_solution(5535414129570525186)
XLA Ops:
  0.0 31.6 %shard_map.37 = f32[3000,128]{1,0:T(8,128)S(1)} custom-call(f32[3,5,10,10,2,384]{5,4,3,2,1,0:T(2,128)} %v_hbm.1, f32[3,3,5,10,10,2,384]{6,5,4,3,2,1,0:T(2,128)} %g_hbm.1, s32[1,384]{1,0:T(1,128)} %place_hbm.1), custom_call_target="tpu_custom_call" | custom-call | tf_op jit(solution)/shard_map/pallas_call | solution.py:741
  31.6 1.1 %copy.7 = f32[10,10,10,1,384]{4,3,2,1,0:T(1,128)} copy(f32[10,10,10,1,384]{4,3,2,1,0:T(1,128)S(1)} %bitcast.1) | data formatting | bytes 3072000

commit v6 on v5

--- a/solution.py
+++ b/solution.py
@@ -11,6 +11,7 @@
 BLOCK_Z = 8
 GRID_Y = 4
 RING_Y = 4
+HELD = 3
 PART_ROWS = ((1, 2, 3), (4, 5, 6, 7, 8, 9, 0))
 PART_INNER = (slice(0, 24), slice(24, 64))
 NODES = 10
@@ -128,14 +129,15 @@
 
     barrier = pltpu.get_barrier_semaphore()
     expected = 2
-    for other in ((elem, o, r), (elem, c, 1 - r)):
-        pl.semaphore_signal(barrier, inc=1, device_id=other, device_id_type=MESH)
-    for neighbour, exists in y_links + x_links:
+    for neighbour, exists in x_links + y_links:
         expected = expected + exists.astype(jnp.int32)
 
         @pl.when(exists)
         def _(neighbour=neighbour):
             pl.semaphore_signal(barrier, inc=1, device_id=neighbour, device_id_type=MESH)
+
+    for other in ((elem, o, r), (elem, c, 1 - r)):
+        pl.semaphore_signal(barrier, inc=1, device_id=other, device_id_type=MESH)
 
     own_copy = pltpu.make_async_copy(place_hbm, place_own, place_sem.at[2])
     own_copy.start()
@@ -264,11 +266,14 @@
         for q in range(2):
             canon[q, a, 64:104] = jnp.dot(parts[q], perm[q], preferred_element_type=jnp.float32)
 
-    def far_first(step, carry):
+    def far_rows(step):
         m = (step + c) % HALF
         mix_planes(m, 0)
         gather_inner(m, far + m, 0)
-        send_inner(far + m, (0,), 0)
+
+    def far_first(step, carry):
+        far_rows(step)
+        send_inner(far + (step + c) % HALF, (0,), 0)
         return carry
 
     def far_second(step, carry):
@@ -280,13 +285,15 @@
         return carry
 
     lax.fori_loop(0, HALF, first_flux(0), 0)
+    far_rows(0)
     pl.semaphore_wait(barrier, expected)
+    send_inner(far + c, (0,), 0)
     place_copy = pltpu.make_async_remote_copy(
         src_ref=place_own, dst_ref=place_in, send_sem=place_sem.at[0], recv_sem=place_sem.at[1],
         device_id=(elem, o, r), device_id_type=MESH,
     )
     place_copy.start()
-    lax.fori_loop(0, HALF, far_first, 0)
+    lax.fori_loop(1, HALF, far_first, 0)
     lax.fori_loop(0, HALF, first_flux(1), 0)
     lax.fori_loop(0, HALF, far_second, 0)
 
@@ -326,7 +333,15 @@
     def near_step(m, carry):
         near_plane(m)
         to_canon(far + m - c, lambda: near_gather(m))
-        send_inner(near + m, (0, 1), 1)
+
+        @pl.when(m != HELD)
+        def _():
+            send_inner(near + m, (0, 1), 1)
+
+        @pl.when(m == HELD)
+        def _():
+            send_inner(near + m, (1,), 2)
+
         return carry
 
     near_plane(0)
@@ -497,16 +512,19 @@
                 out_ref[pl.ds(start, 1), :] = value[first + 32 + number : first + 33 + number, tile(t)]
 
     def inner_wait(group):
-        inner_copy(slice(1, 5), slice(0, 64), group).wait_recv()
+        inner_copy(slice(1, 5 - group), slice(0, 64), group).wait_recv()
+
+    def inner_rows(a, blocks):
+        for t in range(TILES):
+            for b in blocks:
+                rows = slice(b * 8, b * 8 + 8)
+                start = ((a * 10 + b + 1) * 10 + 1) * 3 + t
+                out_ref[pl.ds(start, 8, stride=3), :] = got[a, rows, tile(t)] + raw[c, a, rows, tile(t)]
 
     def inner_done(a, carry):
-        @pl.when(is_inner(a))
+        @pl.when(jnp.logical_and(is_inner(a), a != far + HELD))
         def _():
-            for t in range(TILES):
-                value = got[a, 0:64, tile(t)] + raw[c, a, 0:64, tile(t)]
-                for b in range(8):
-                    start = ((a * 10 + b + 1) * 10 + 1) * 3 + t
-                    out_ref[pl.ds(start, 8, stride=3), :] = value[b * 8 : b * 8 + 8]
+            inner_rows(a, range(8))
 
         return carry
 
@@ -660,8 +678,11 @@
     fill_ends(8, 3, 32)
     x_tops.start()
     x_ends.start()
+    inner_copy(near + HELD, PART_INNER[0], 3).start()
     inner_wait(1)
     lax.fori_loop(far, far + HALF, inner_done, 0)
+    inner_copy(far + HELD, PART_INNER[1], 2).wait_recv()
+    inner_rows(far + HELD, range(3, 8))
 
     def complete(a, carry):
         for t in range(TILES):
@@ -718,6 +739,9 @@
     value = permuted(total, back[...])
     for k, a in enumerate((0, 9)):
         put_edges(a, value, k * 40)
+
+    inner_copy(far + HELD, PART_INNER[0], 3).wait_recv()
+    inner_rows(far + HELD, range(3))
 
     z_copy(2).wait_send()
     for way in range(2):
@@ -772,7 +796,7 @@
             vmem((56, LANES), f32),
             vmem((56, LANES), f32),
             dma((2, HALF)), dma((HALF,)), dma((3,)), dma((3,)), dma((3, 2)), dma((2, 2)),
-            dma((4,)), dma((2,)), dma((3,)),
+            dma((4,)), dma((4,)), dma((3,)),
         ],
         compiler_params=pltpu.CompilerParams(
             collective_id=0, has_side_effects=True, vmem_limit_bytes=60 * 1024 * 1024

time: 32.9 us -> 32.5 us (0.988)
  Pallas kernels: 31.6 us -> 31.2 us
    pallas_call x1, Pallas kernels: 31.6 us -> 31.2 us  [body(): pl.pallas_call(kernel, out_shape=pltpu.VMEM((NODES * NODES * NODES * TILE...]
where the time goes in v6:
time: 32.5 us; the launch traced here: 32.4 us
  Pallas kernels  31.2 us (96%)
  local copies, waits for them, and re-layouts  1.13 us (3%)
    pallas_call x1, Pallas kernels, body(): pl.pallas_call(kernel, out_shape=pltpu.VMEM((NODES * NODES * NODES * TILE...  31.2 us
    unnamed x1, local copies, waits for them, and re-layouts  1.13 us

profile of v6, /device:TPU:1, one launch (start us, length us, event | category | flops | bytes accessed | tf_op | source)
XLA Modules:
  0.0 32.4 jit_solution(2828977618856391573)
XLA Ops:
  0.0 31.2 %shard_map.37 = f32[3000,128]{1,0:T(8,128)S(1)} custom-call(f32[3,5,10,10,2,384]{5,4,3,2,1,0:T(2,128)} %v_hbm.1, f32[3,3,5,10,10,2,384]{6,5,4,3,2,1,0:T(2,128)} %g_hbm.1, s32[1,384]{1,0:T(1,128)} %place_hbm.1), custom_call_target="tpu_custom_call" | custom-call | tf_op jit(solution)/shard_map/pallas_call | solution.py:765
  31.2 1.1 %copy.7 = f32[10,10,10,1,384]{4,3,2,1,0:T(1,128)} copy(f32[10,10,10,1,384]{4,3,2,1,0:T(1,128)S(1)} %bitcast.1) | data formatting | bytes 3072000

commit v7 on v6

--- a/solution.py
+++ b/solution.py
@@ -112,7 +112,7 @@
     v_hbm, g_hbm, place_hbm, out_ref,
     v, g, coef, f0, fl, fn, perm, back, place_own, place_in, raw, canon, got,
     zs, zr, ys, yr, xs, xr, tops, tops_in, ends, ends_in,
-    first_sem, later_sem, place_sem, z_sem, y_sem, x_sem, send_sem, inner_sem, edge_sem,
+    first_sem, place_sem, z_sem, y_sem, x_sem, send_sem, inner_sem, edge_sem,
 ):
     elem = lax.axis_index("elem")
     c = lax.axis_index("comp")
@@ -156,7 +156,7 @@
         pltpu.make_async_copy(g_hbm.at[:, 0:2, i, here], g.at[:, 0:2, i, here], first_sem.at[part, i]).wait()
 
     def later_copy(i):
-        return pltpu.make_async_copy(g_hbm.at[:, 1:3, i], g.at[:, 1:3, i], later_sem.at[i])
+        return pltpu.make_async_copy(g_hbm.at[:, 1:3, i], g.at[:, 1:3, i], first_sem.at[0, i])
 
     for i in range(HALF):
         for copy in first_copies(i, 0):
@@ -176,7 +176,6 @@
                 coef[(kind * HALF + m) * HALF + i] = jnp.where(c == 0, first, second).astype(jnp.float32)
 
 
-    own_copy.wait()
     rows_iota = lax.broadcasted_iota(jnp.int32, (ELEMS, ELEMS), 0)
     lanes_iota = lax.broadcasted_iota(jnp.int32, (LANES, ELEMS), 1).astype(jnp.float32)
 
@@ -188,10 +187,6 @@
             for copy in range(2):
                 perm[q, copy * ELEMS + t * LANES : copy * ELEMS + (t + 1) * LANES, :] = part
 
-    back_half = jnp.where(rows_iota == place_own[...], 1.0, 0.0).astype(jnp.bfloat16)
-    back[0:ELEMS, :] = back_half
-    back[ELEMS : 2 * ELEMS, :] = back_half
-    fill_perm(c, place_own[...])
     raw[:, :, 96:104] = jnp.zeros((2, NODES, 8, ELEMS), jnp.float32)
 
     far = HALF * o
@@ -284,8 +279,13 @@
         gather_edges(m, far + m)
         return carry
 
+    fl[0] = jnp.zeros(fl.shape[1:], jnp.float32)
+    gather_inner(0, 0, 0)
+    gather_inner(0, 0, 1)
+    gather_edges(0, 0)
     lax.fori_loop(0, HALF, first_flux(0), 0)
     far_rows(0)
+    own_copy.wait()
     pl.semaphore_wait(barrier, expected)
     send_inner(far + c, (0,), 0)
     place_copy = pltpu.make_async_remote_copy(
@@ -348,6 +348,10 @@
     near_gather(0)
     send_inner(near, (0, 1), 1)
     place_copy.wait()
+    back_half = jnp.where(rows_iota == place_own[...], 1.0, 0.0).astype(jnp.bfloat16)
+    back[0:ELEMS, :] = back_half
+    back[ELEMS : 2 * ELEMS, :] = back_half
+    fill_perm(c, place_own[...])
     fill_perm(o, place_in[...])
     lax.fori_loop(1, HALF, near_step, 0)
     six_planes = pl.ds(near - c, HALF + 1)
@@ -444,7 +448,7 @@
     def z_copy(part):
         here = (slice(0, 8), slice(8, 10), slice(0, 10))[part]
         return pltpu.make_async_remote_copy(
-            src_ref=zs.at[:, here], dst_ref=zr.at[:, here], send_sem=z_sem.at[2], recv_sem=z_sem.at[part % 2],
+            src_ref=zs.at[:, here], dst_ref=zr.at[:, here], send_sem=first_sem.at[1, 4], recv_sem=z_sem.at[part % 2],
             device_id=(elem, c, 1 - r), device_id_type=MESH,
         )
 
@@ -458,7 +462,7 @@
 
     def x_copy(way):
         return pltpu.make_async_remote_copy(
-            src_ref=xs.at[way], dst_ref=xr.at[way], send_sem=x_sem.at[0, way], recv_sem=x_sem.at[1, way],
+            src_ref=xs.at[way], dst_ref=xr.at[way], send_sem=first_sem.at[1, way], recv_sem=x_sem.at[way],
             device_id=x_links[way][0], device_id_type=MESH,
         )
 
@@ -466,7 +470,7 @@
         here = (slice(0, 80), slice(80, ROWS), slice(0, ROWS))[part]
         return pltpu.make_async_remote_copy(
             src_ref=ys.at[way, here], dst_ref=yr.at[way, here],
-            send_sem=y_sem.at[2, way], recv_sem=y_sem.at[part % 2, way],
+            send_sem=first_sem.at[1, 2 + way], recv_sem=y_sem.at[part % 2, way],
             device_id=y_links[way][0], device_id_type=MESH,
         )
 
@@ -795,7 +799,7 @@
             vmem((NODES - 1, 16, LANES), f32),
             vmem((56, LANES), f32),
             vmem((56, LANES), f32),
-            dma((2, HALF)), dma((HALF,)), dma((3,)), dma((3,)), dma((3, 2)), dma((2, 2)),
+            dma((2, HALF)), dma((3,)), dma((2,)), dma((2, 2)), dma((2,)),
             dma((4,)), dma((4,)), dma((3,)),
         ],
         compiler_params=pltpu.CompilerParams(

time: 32.5 us -> 32.1 us (0.988)
  Pallas kernels: 31.2 us -> 30.8 us
    pallas_call x1, Pallas kernels: 31.2 us -> 30.8 us  [body(): pl.pallas_call(kernel, out_shape=pltpu.VMEM((NODES * NODES * NODES * TILE...]
where the time goes in v7:
time: 32.1 us; the launch traced here: 31.9 us
  Pallas kernels  30.8 us (96%)
  local copies, waits for them, and re-layouts  1.13 us (4%)
    pallas_call x1, Pallas kernels, body(): pl.pallas_call(kernel, out_shape=pltpu.VMEM((NODES * NODES * NODES * TILE...  30.8 us
    unnamed x1, local copies, waits for them, and re-layouts  1.13 us

profile of v7, /device:TPU:1, one launch (start us, length us, event | category | flops | bytes accessed | tf_op | source)
XLA Modules:
  0.0 31.9 jit_solution(7705174175653378142)
XLA Ops:
  0.0 30.8 %shard_map.37 = f32[3000,128]{1,0:T(8,128)S(1)} custom-call(f32[3,5,10,10,2,384]{5,4,3,2,1,0:T(2,128)} %v_hbm.1, f32[3,3,5,10,10,2,384]{6,5,4,3,2,1,0:T(2,128)} %g_hbm.1, s32[1,384]{1,0:T(1,128)} %place_hbm.1), custom_call_target="tpu_custom_call" | custom-call | tf_op jit(solution)/shard_map/pallas_call | solution.py:769
  30.8 1.1 %copy.7 = f32[10,10,10,1,384]{4,3,2,1,0:T(1,128)} copy(f32[10,10,10,1,384]{4,3,2,1,0:T(1,128)S(1)} %bitcast.1) | data formatting | bytes 3072000
